TPU v7x, 32 devices: a whole 2x2x4 slice. The times are simulated.
32 devices in a mesh: row: 4 (over y, x), col: 8 (over z, core).
Axes of the slice: x: 2, y: 2, z: 4, core: 2. Of those that a mesh axis runs over, the one named last changes fastest.
Arguments:
- diag_inverse: bfloat16 [1376, 1376], P('row'), may hold values from -0.5 to 0.5, as said below
- row_u: bfloat16 [4, 1376, 224], P('row', None, 'col'), may hold values from -6 to 6
- row_v: bfloat16 [4, 1376, 224], P('row', None, 'col'), may hold values from -0.59765625 to 0.59765625
- col_u: bfloat16 [8, 1376, 224], P('col', None, 'row'), may hold values from -6 to 6
- col_v: bfloat16 [8, 1376, 224], P('col', None, 'row'), may hold values from -0.59765625 to 0.59765625
- tile_u: bfloat16 [4, 8, 1376, 224], P('row', 'col'), may hold values from -6 to 6
- tile_v: bfloat16 [4, 8, 1376, 224], P('row', 'col'), may hold values from -6 to 6
- sketch: bfloat16 [1376, 224], replicated, may hold values from -6 to 6
- row_rank: int32 [4], P('row'), may hold values from 56 to 224, as said below
- col_rank: int32 [8], P('col'), may hold values from 56 to 224, as said below
- old_rank: int32 [4, 8], P('row', 'col'), may hold values from 56 to 224, as said below
- new_rank: int32 [4, 8], P('row', 'col'), may hold values from 14 to 112, as said below
Outputs:
- new_u: bfloat16 [4, 8, 1376, 224], P('row', 'col')
- new_v: bfloat16 [4, 8, 1376, 224], P('row', 'col')
Inputs may be any that keep to these rules, and one draw needn't show every extreme that they name: diag_inverse is lower triangular with diagonal entries between 0.25 and 0.5. `row_rank`: some tile has rank 224. `col_rank`: some tile has rank 224. `old_rank`: some tile has rank 224. `new_rank`: each entry lies between old_rank // 4 and old_rank // 2 of the same tile; some tile has rank 224 // 2.
All inputs are finite; a program needn't handle non-finite values.
Results may differ from a plain program's by a relative error of at most 0.0085.
Values may be sent and summed in bfloat16 or wider, within the bound.
No kernel may reach another device: no remote copies, remote signals or barrier semaphores. Data moves between devices by JAX's collectives and lax.ppermute only.
A program may use at most 64 MiB of HBM per device.

v0:
```python
import jax
import jax.numpy as jnp
from jax import lax
from jax.sharding import PartitionSpec as P

precise_mode = lax.Precision.HIGHEST


def keep_mask(rank_cap, count):
    return jnp.arange(rank_cap, dtype=jnp.int32) < count


def solve_share(inverse, right_side, count):
    rank_cap = right_side.shape[2]
    keep_cols = jnp.arange(rank_cap, dtype=jnp.int32) < count
    values = jnp.where(keep_cols[None, :], right_side[0], jnp.zeros_like(right_side[0]))
    solved = jnp.dot(inverse, values, preferred_element_type=jnp.float32)
    return solved.astype(jnp.bfloat16)[None]


def tile_update(base_u, base_v, left_u, left_w, right_u, right_w, sketch, old_count, new_count):
    row_count, rank_cap = base_u.shape
    kept_v = jnp.where(keep_mask(rank_cap, old_count)[None, :], base_v, jnp.zeros_like(base_v))
    new_keep = keep_mask(rank_cap, new_count)
    probe_cols = jnp.where(new_keep[None, :], sketch, jnp.zeros_like(sketch))
    core_mat = jnp.dot(left_w.T, right_w, preferred_element_type=jnp.float32).astype(jnp.bfloat16)
    left_small = jnp.dot(kept_v.T, probe_cols, preferred_element_type=jnp.float32).astype(
        jnp.bfloat16
    )
    across = jnp.dot(right_u.T, probe_cols, preferred_element_type=jnp.float32).astype(jnp.bfloat16)
    middle = jnp.dot(core_mat, across, preferred_element_type=jnp.float32).astype(jnp.bfloat16)
    range_y = jnp.dot(base_u, left_small, preferred_element_type=jnp.float32) - jnp.dot(
        left_u, middle, preferred_element_type=jnp.float32
    )
    padding = jnp.where(new_keep, 0.0, 1.0).astype(jnp.float32)
    gram = jnp.dot(
        range_y.T, range_y, precision=precise_mode, preferred_element_type=jnp.float32
    ) + jnp.diag(padding)
    gram_factor = jnp.linalg.cholesky(gram)
    range_basis = jax.scipy.linalg.solve_triangular(gram_factor, range_y.T, lower=True).T
    new_u = (jnp.sqrt(jnp.float32(row_count)) * range_basis).astype(jnp.bfloat16)
    back_small = jnp.dot(base_u.T, new_u, preferred_element_type=jnp.float32).astype(jnp.bfloat16)
    side_small = jnp.dot(left_u.T, new_u, preferred_element_type=jnp.float32).astype(jnp.bfloat16)
    turned = jnp.dot(core_mat.T, side_small, preferred_element_type=jnp.float32).astype(
        jnp.bfloat16
    )
    summed = jnp.dot(kept_v, back_small, preferred_element_type=jnp.float32) - jnp.dot(
        right_u, turned, preferred_element_type=jnp.float32
    )
    new_v = (summed / jnp.float32(row_count)).astype(jnp.bfloat16)
    return (new_u, new_v)


def on_device(
    diag_inverse,
    row_u,
    row_v,
    col_u,
    col_v,
    tile_u,
    tile_v,
    sketch,
    row_rank,
    col_rank,
    old_rank,
    new_rank,
):
    inverse = lax.all_gather(diag_inverse, "row", axis=0, tiled=True)
    row_basis, row_right = (
        lax.all_gather(row_u, "col", axis=2, tiled=True),
        lax.all_gather(row_v, "col", axis=2, tiled=True),
    )
    row_right = solve_share(inverse, row_right, row_rank[0])
    col_basis, col_right = (
        lax.all_gather(col_u, "row", axis=2, tiled=True),
        lax.all_gather(col_v, "row", axis=2, tiled=True),
    )
    col_right = solve_share(inverse, col_right, col_rank[0])
    new_u, new_v = tile_update(
        tile_u[0, 0],
        tile_v[0, 0],
        row_basis[0],
        row_right[0],
        col_basis[0],
        col_right[0],
        sketch,
        old_rank[0, 0],
        new_rank[0, 0],
    )
    return (new_u[None, None], new_v[None, None])


def solution(mesh):
    in_specs = (
        P("row", None),
        P("row", None, "col"),
        P("row", None, "col"),
        P("col", None, "row"),
        P("col", None, "row"),
        P("row", "col", None, None),
        P("row", "col", None, None),
        P(),
        P("row"),
        P("col"),
        P("row", "col"),
        P("row", "col"),
    )
    out_specs = (P("row", "col", None, None), P("row", "col", None, None))
    return jax.shard_map(
        on_device, mesh=mesh, in_specs=in_specs, out_specs=out_specs, check_vma=False
    )
```

profile of v0, /device:TPU:0, one launch (start us, length us, event | category | flops | bytes accessed | tf_op | source)
XLA Modules:
  0.0 164.7 jit_solution(14733544802278517896)
XLA Ops:
  7.2 0.0 copy-start
  7.2 0.0 copy-start.8
  7.2 0.0 copy-start.6
  7.2 0.0 copy-start.7
  7.2 0.0 all-gather.2.cloned.1.call-start
  7.3 0.7 all-gather.2.cloned.1.call-update
  7.9 0.0 copy-start.5
  10.0 1.0 copy.22
  11.6 0.0 copy-done.8
  11.6 0.1 copy.23
  11.8 0.0 copy-done.6
  11.9 16.2 %all_gather.17 = bf16[1,1376,224]{1,2,0:T(8,128)(2,1)} all-gather(bf16[1,1376,56]{1,2,0:T(8,128)(2,1)S(1)} %copy-done.6), channel_id=1, replica_groups=mesh['row'=4,'col'=8] {'row'}, dimensions={2}, use_global_device_ids=true | all-gather | bytes 770560 | tf_op jit(solution)/shard_map/all_gather | solution.py:76
  28.1 0.0 copy-done.7
  28.1 13.0 %all_gather.18 = bf16[1,1376,224]{1,2,0:T(8,128)(2,1)S(1)} all-gather(bf16[1,1376,56]{1,2,0:T(8,128)(2,1)S(1)} %copy-done.7), channel_id=1, replica_groups=mesh['row'=4,'col'=8] {'row'}, dimensions={2}, use_global_device_ids=true | all-gather | bytes 770560 | tf_op jit(solution)/shard_map/all_gather | solution.py:75
  41.0 0.0 copy-done.5
  41.0 0.4 convolution_convert_fusion.2
  41.4 0.0 copy-start.1
  41.4 19.2 %all_gather.15 = bf16[1,1376,224]{1,0,2:T(2,128)(2,1)} all-gather(bf16[1,1376,28]{1,0,2:T(2,128)(2,1)S(1)} %copy.22), channel_id=1, replica_groups=mesh['row'=4,'col'=8] {'col'}, dimensions={2}, use_global_device_ids=true | all-gather | bytes 693504 | tf_op jit(solution)/shard_map/all_gather | solution.py:71
  60.6 0.0 copy-done.3
  60.6 18.3 %all_gather.19 = bf16[1,1376,224]{1,0,2:T(2,128)(2,1)} all-gather(bf16[1,1376,28]{1,0,2:T(2,128)(2,1)S(1)} %copy.23), channel_id=1, replica_groups=mesh['row'=4,'col'=8] {'col'}, dimensions={2}, use_global_device_ids=true | all-gather | bytes 693504 | tf_op jit(solution)/shard_map/all_gather | solution.py:70
  78.9 0.0 copy-done
  78.9 0.0 copy-done.1
  78.9 1.1 fusion.4
  80.0 0.0 copy-start.4
  80.0 0.0 all-gather.2.cloned.1.call-done
  80.0 4.7 %convolution_convert_fusion = bf16[224,1376]{1,0:T(8,128)(2,1)} fusion(bf16[1376,1376]{1,0:T(8,128)(2,1)} %all-gather.2.cloned.1.call-done, bf16[1,1376,224]{1,2,0:T(8,128)(2,1)} %all_gather.17, pred[224]{0:T(512)(128)(4,1)S(1)} %iota_compare_fusion.8), kind=kOutput, calls=%fused_computation.5 | convolution fusion | flops 848848896 | bytes 5019872 | tf_op jit(solution)/shard_map/dot_general | solution.py:17
  84.7 4.0 %convolution_convert_fusion.3 = bf16[224,224]{1,0:T(8,128)(2,1)S(1)} fusion(bf16[224,1376]{1,0:T(8,128)(2,1)} %convolution_convert_fusion, bf16[1376,1376]{1,0:T(8,128)(2,1)} %all-gather.2.cloned.1.call-done, bf16[1,1376,224]{1,0,2:T(2,128)(2,1)S(1)} %copy-done.4, pred[224]{0:T(512)(128)(4,1)S(1)} %iota_compare_fusion.9), kind=kOutput, calls=%fused_computation.12 | convolution fusion | flops 986983424 | bytes 5120224 | tf_op jit(solution)/shard_map/dot_general | solution.py:26
  88.7 1.9 %convolution_subtract_fusion.1 = f32[224,1376]{1,0:T(8,128)S(1)} fusion(f32[224,1376]{1,0:T(8,128)S(1)} %fusion.4, bf16[224,224]{1,0:T(8,128)(2,1)S(1)} %convolution_convert_fusion.3, bf16[224,224]{1,0:T(8,128)(2,1)S(1)} %convolution_convert_fusion.2, bf16[1,1376,224]{1,0,2:T(2,128)(2,1)} %all_gather.19), kind=kOutput, calls=%fused_computation.1 | convolution fusion | flops 160921600 | bytes 3282944 | tf_op jit(solution)/shard_map/dot_general | solution.py:32
  90.7 1.3 fusion.46
  91.9 0.1 copy.24
  92.1 0.1 fusion.27
  92.2 11.7 %cholesky.50 = f32[128,128]{1,0:T(8,128)S(1)} custom-call(f32[128,128]{1,0:T(8,128)S(1)} %cholesky.121), custom_call_target="Cholesky" | custom-call | tf_op jit(solution)/shard_map/jit(cholesky)/cholesky | solution.py:39
  104.0 9.8 %custom-call.15 = f32[1,128,128]{1,2,0:T(8,128)S(1)} custom-call(f32[1,128,128]{2,1,0:T(8,128)S(1)} %get-tuple-element.29), custom_call_target="InvertDiagBlocksLowerTriangular" | custom-call | tf_op jit(solution)/shard_map/jit(cholesky)/cholesky | solution.py:39
  113.8 0.4 constant_dynamic-update-slice_fusion.1
  114.1 0.2 convolution_subtract_fusion.3
  114.4 8.8 %cholesky.108 = f32[96,96]{1,0:T(8,128)S(1)} custom-call(f32[96,96]{1,0:T(8,128)S(1)} %convolution_subtract_fusion.3), custom_call_target="Cholesky" | custom-call | tf_op jit(solution)/shard_map/jit(cholesky)/cholesky | solution.py:39
  123.2 0.6 compare_reduce_fusion.1
  123.8 0.6 compare_reduce_fusion
  125.8 0.1 fusion.28
  125.9 19.7 %custom-call.16 = f32[2,128,128]{1,2,0:T(8,128)S(1)} custom-call(f32[2,128,128]{2,1,0:T(8,128)S(1)} %pad_maximum_fusion), custom_call_target="InvertDiagBlocksLowerTriangular" | custom-call | tf_op jit(solution)/shard_map/jit(_solve_triangular)/triangular_solve | solution.py:40
  145.6 1.3 fusion.5
  146.9 0.8 convolution_subtract_fusion.2
  147.7 1.3 fusion.32
  149.0 0.2 fusion.45
  149.2 1.9 %convolution_convert_fusion.7 = bf16[224,224]{1,0:T(8,128)(2,1)S(1)} fusion(bf16[224,224]{1,0:T(8,128)(2,1)S(1)} %convolution_convert_fusion.3, bf16[1,1376,224]{1,0,2:T(2,128)(2,1)} %all_gather.19, f32[96,1376]{0,1:T(8,128)S(1)} %fusion.32, f32[128,1376]{0,1:T(8,128)S(1)} %fusion.5), kind=kOutput, calls=%fused_computation.16 | convolution fusion | flops 161588224 | bytes 2050048 | tf_op jit(solution)/shard_map/dot_general | solution.py:44
  151.1 1.1 copy.26
  152.2 2.6 %convolution_bitcast_fusion = f32[1376,224]{0,1:T(8,128)} fusion(bf16[224,224]{1,0:T(8,128)(2,1)S(1)} %convolution_convert_fusion.7, bf16[1,1376,224]{1,2,0:T(8,128)(2,1)} %copy-done.3), kind=kOutput, calls=%fused_computation.3 | convolution fusion | flops 138084352 | bytes 1949696 | tf_op jit(solution)/shard_map/dot_general | solution.py:47
  154.8 3.1 %fusion.2 = bf16[1,1,1376,224]{2,3,1,0:T(8,128)(2,1)} fusion(f32[1376,224]{0,1:T(8,128)} %convolution_bitcast_fusion, bf16[1,1,1376,224]{2,3,1,0:T(8,128)(2,1)S(1)} %copy-done, bf16[1,1,1376,224]{2,3,1,0:T(8,128)(2,1)S(1)} %copy-done.2, pred[224]{0:T(512)(128)(4,1)S(1)} %get-tuple-element.35, f32[96,1376]{0,1:T(8,128)S(1)} %fusion.32, f32[128,1376]{0,1:T(8,128)S(1)} %fusion.5), kind=kOutput, calls=%fused_computation.7 | convolution fusion | flops 278376448 | bytes 4315360 | tf_op jit(solution)/shard_map/dot_general | solution.py:47
  (18 shorter events, 0.2 us)
Async XLA Ops:
  7.2 71.7 %copy-start = (bf16[1,1,1376,224]{2,3,1,0:T(8,128)(2,1)S(1)}, bf16[1,1,1376,224]{2,3,1,0:T(8,128)(2,1)}, u32[]{:S(2)}) copy-start(bf16[1,1,1376,224]{2,3,1,0:T(8,128)(2,1)} %param.17) | copy-start | bytes 1849348
  7.2 4.4 %copy-start.8 = (bf16[1,1376,28]{1,2,0:T(8,128)(2,1)S(1)}, bf16[1,1376,28]{1,2,0:T(8,128)(2,1)}, u32[]{:S(2)}) copy-start(bf16[1,1376,28]{1,2,0:T(8,128)(2,1)} %param.13) | copy-start | bytes 231172
  7.2 4.7 %copy-start.6 = (bf16[1,1376,56]{1,2,0:T(8,128)(2,1)S(1)}, bf16[1,1376,56]{1,2,0:T(8,128)(2,1)}, u32[]{:S(2)}) copy-start(bf16[1,1376,56]{1,2,0:T(8,128)(2,1)} %param.16) | copy-start | bytes 462340
  7.2 20.9 %copy-start.7 = (bf16[1,1376,56]{1,2,0:T(8,128)(2,1)S(1)}, bf16[1,1376,56]{1,2,0:T(8,128)(2,1)}, u32[]{:S(2)}) copy-start(bf16[1,1376,56]{1,2,0:T(8,128)(2,1)} %param.15) | copy-start | bytes 462340
  7.2 72.8 %all-gather.2.cloned.1.call-start = ((), (), s32[]{:S(2)}) async-start(), calls=%async_computation | async-start | bytes 4843520 | tf_op jit(solution)/shard_map/all_gather | solution.py:68
  7.9 33.1 %copy-start.5 = (bf16[1376,224]{0,1:T(8,128)(2,1)S(1)}, bf16[1376,224]{0,1:T(8,128)(2,1)}, u32[]{:S(2)}) copy-start(bf16[1376,224]{0,1:T(8,128)(2,1)} %param.19) | copy-start | bytes 1849348
  41.0 19.6 %copy-start.3 = (bf16[1,1376,224]{1,2,0:T(8,128)(2,1)}, bf16[1,1376,224]{1,2,0:T(8,128)(2,1)S(1)}, u32[]{:S(2)}) copy-start(bf16[1,1376,224]{1,2,0:T(8,128)(2,1)S(1)} %all_gather.18) | copy-start | bytes 1849348
  41.4 37.4 %copy-start.1 = (bf16[1,1,1376,224]{2,3,1,0:T(8,128)(2,1)S(1)}, bf16[1,1,1376,224]{2,3,1,0:T(8,128)(2,1)}, u32[]{:S(2)}) copy-start(bf16[1,1,1376,224]{2,3,1,0:T(8,128)(2,1)} %param.18) | copy-start | bytes 1849348
  80.0 4.7 %copy-start.4 = (bf16[1,1376,224]{1,0,2:T(2,128)(2,1)S(1)}, bf16[1,1376,224]{1,0,2:T(2,128)(2,1)}, u32[]{:S(2)}) copy-start(bf16[1,1376,224]{1,0,2:T(2,128)(2,1)} %all_gather.15) | copy-start | bytes 1849348
  152.2 2.6 %copy-start.2 = (bf16[1,1,1376,224]{2,3,1,0:T(8,128)(2,1)S(1)}, bf16[1,1,1376,224]{2,3,1,0:T(8,128)(2,1)}, u32[]{:S(2)}) copy-start(bf16[1,1,1376,224]{2,3,1,0:T(8,128)(2,1)} %param.18) | copy-start | bytes 1849348
Sparse Core Ops, SparseCore 0:
  9.9 57.1 all-gather.1
where the time goes:
time: 165 us
  blocking collectives  66.6 us (40%)
  other arithmetic  51.8 us (31%)
  matrix products  24.9 us (15%)
  between operations  18.3 us (11%)
  local copies, waits for them, and re-layouts  2.43 us (1%)
    another operation x7, other arithmetic, tile_update(): gram_factor = jnp.linalg.cholesky(gram)  31.6 us
    another operation x6, other arithmetic, tile_update(): jax.scipy.linalg.solve_triangular(gram_factor, range_y.T, lower=True)  19.8 us
    all_gather x1, blocking collectives, on_device(): lax.all_gather(row_v, 'col', axis=2, tiled=True)  19.2 us
    all_gather x1, blocking collectives, on_device(): lax.all_gather(row_u, 'col', axis=2, tiled=True)  18.3 us
    all_gather x1, blocking collectives, on_device(): lax.all_gather(col_v, 'row', axis=2, tiled=True)  16.2 us
    all_gather x1, blocking collectives, on_device(): lax.all_gather(col_u, 'row', axis=2, tiled=True)  13 us
    dot_general x1, matrix products, solve_share(): solved = jnp.dot(inverse, values, preferred_element_type=jnp.float32)  4.65 us
    dot_general x1, matrix products, tile_update(): jnp.dot(left_w.T, right_w, preferred_element_type=jnp.float32)  4.03 us
  transfers between devices with their start and end apart: 1, of which 0 were waited for; matrix products, arithmetic and copies ran while one was open for 2% of the time, Pallas kernels for 0%

commit v1 on v0

v1 whole, which is shorter than its diff:
```python
import functools

import jax
import jax.numpy as jnp
from jax import lax
from jax.experimental import pallas as pl
from jax.experimental.pallas import tpu as pltpu
from jax.sharding import PartitionSpec as P

FULL = lax.Precision.HIGHEST
NT = (((1,), (1,)), ((), ()))
NN = (((1,), (0,)), ((), ()))
LANES = 128
SUBLANES = 8
PACK = 16


def dot_nt(a, b, precision=None):
    return lax.dot_general(a, b, NT, precision=precision, preferred_element_type=jnp.float32)


def dot_nn(a, b, precision=None):
    return lax.dot_general(a, b, NN, precision=precision, preferred_element_type=jnp.float32)


def round_up(n, m):
    return (n + m - 1) // m * m


def by_pairs(n):
    return n <= 8 and n & (n - 1) == 0


def swap(x, axis, n, k):
    return lax.ppermute(x, axis, [(i, i ^ k) for i in range(n)])


def spread(x, axis, n):
    if n == 1:
        return [x]
    if by_pairs(n):
        return [x] + [swap(x, axis, n, k) for k in range(1, n)]
    every = lax.all_gather(x, axis)
    return [every[k] for k in range(n)]


def spread_near(x, axis, n):
    if n < 4 or not by_pairs(n):
        return spread(x, axis, n)
    even = [x] + [swap(x, axis, n, k) for k in range(2, n, 2)]
    odd = [swap(e, axis, n, 1) for e in even]
    return [(odd if k % 2 else even)[k // 2] for k in range(n)]


def hand_out(parts, axis, n):
    if n == 1:
        return parts
    if by_pairs(n):
        return [parts[0]] + [swap(parts[k], axis, n, k) for k in range(1, n)]
    got = lax.all_to_all(jnp.stack(parts), axis, 0, 0)
    return [got[k] for k in range(n)]


def source_of(own, k, n):
    return own ^ k if by_pairs(n) else k


def call(body, out_shape, n_smem, n_vmem, scratch=()):
    return pl.pallas_call(
        body,
        out_shape=out_shape,
        in_specs=[pl.BlockSpec(memory_space=pltpu.SMEM)] * n_smem
        + [pl.BlockSpec(memory_space=pltpu.VMEM)] * n_vmem,
        scratch_shapes=list(scratch),
        compiler_params=pltpu.CompilerParams(vmem_limit_bytes=56 * 1024 * 1024),
    )


def row_solve_body(*refs, pad):
    *chunks, inverse, out, stacked = refs
    stacked[...] = jnp.zeros_like(stacked)
    width = chunks[0].shape[0]
    for k, chunk in enumerate(chunks):
        stacked[k * pad : k * pad + width, :] = chunk[...]
    out[...] = dot_nt(stacked[...], inverse[...]).astype(jnp.bfloat16)


def core_body(*refs, n_row, n_col, row_pad, col_pad):
    own, refs = refs[0], refs[1:]
    col_chunks, refs = refs[:n_row], refs[n_row:]
    inverse, refs = refs[0], refs[1:]
    solved, refs = refs[:n_col], refs[n_col:]
    outs, stacked = refs[:n_row], refs[n_row]
    stacked[...] = jnp.zeros_like(stacked)
    width = col_chunks[0].shape[0]
    for k, chunk in enumerate(col_chunks):
        at = source_of(own[0], k, n_row)
        stacked[pl.ds(pl.multiple_of(at * col_pad, col_pad), width), :] = chunk[...]
    col_solved = dot_nt(stacked[...], inverse[...]).astype(jnp.bfloat16)
    for m in range(n_col):
        part = dot_nt(solved[m][...], col_solved).astype(jnp.bfloat16)
        for k in range(n_row):
            outs[k][m * row_pad : (m + 1) * row_pad, :] = part[k * row_pad : (k + 1) * row_pad, :]


def lane_spread(x, lane):
    return jnp.broadcast_to(x[:, lane : lane + 1], x.shape)


def row_spread(x, row):
    return jnp.broadcast_to(x[row : row + 1, :], x.shape)


def inverse_factor(gram, live):
    size = gram.shape[0]
    blocks = size // SUBLANES
    live_blocks = live // SUBLANES if live % SUBLANES == 0 else blocks
    sub = lax.broadcasted_iota(jnp.int32, (SUBLANES, size), 0)
    lane = lax.broadcasted_iota(jnp.int32, (SUBLANES, size), 1)
    left = [gram[i * SUBLANES : (i + 1) * SUBLANES, :] for i in range(blocks)]
    right = [jnp.where(lane == sub + i * SUBLANES, 1.0, 0.0).astype(jnp.float32) for i in range(blocks)]
    for b in range(live_blocks):
        cols = {
            (i, q): lane_spread(left[i], b * SUBLANES + q)
            for i in range(b, live_blocks)
            for q in range(SUBLANES)
        }
        scale = jnp.zeros((SUBLANES, size), jnp.float32)
        for q in range(SUBLANES):
            root = lax.rsqrt(row_spread(cols[b, q], q))
            scale = jnp.where(sub == q, root, scale)
            square = root * root
            left_row = row_spread(left[b], q)
            right_row = row_spread(right[b], q)
            heads = {p: row_spread(cols[b, p], q) for p in range(q + 1, SUBLANES)}
            for i in range(b, live_blocks):
                times = cols[i, q] * square
                if i == b:
                    times = jnp.where(sub > q, times, 0.0)
                left[i] = left[i] - times * left_row
                right[i] = right[i] - times * right_row
                for p in range(q + 1, SUBLANES):
                    cols[i, p] = cols[i, p] - times * heads[p]
        right[b] = right[b] * scale
    return jnp.concatenate(right, axis=0)


def tile_body(*refs, n_row, n_col, row_pad, col_pad, half):
    (own_col, own_row, row_rank, col_rank, old_rank, new_rank), refs = refs[:6], refs[6:]
    cores, refs = refs[:n_row], refs[n_row:]
    row_chunks, refs = refs[:n_col], refs[n_col:]
    col_chunks, refs = refs[:n_row], refs[n_row:]
    base_u, base_v, sketch, new_u, new_v, left_u, right_u = refs
    rank_cap, row_count = base_u.shape
    row_width, col_width = row_chunks[0].shape[0], col_chunks[0].shape[0]
    n_p, n_q = n_col * row_pad, n_row * col_pad

    left_u[...] = jnp.zeros_like(left_u)
    for m, chunk in enumerate(row_chunks):
        left_u[m * row_pad : m * row_pad + row_width, :] = chunk[...]
    right_u[...] = jnp.zeros_like(right_u)
    for k, chunk in enumerate(col_chunks):
        at = source_of(own_row[0], k, n_row)
        right_u[pl.ds(pl.multiple_of(at * col_pad, col_pad), col_width), :] = chunk[...]

    total = cores[0][...].astype(jnp.float32)
    for k in range(1, n_row):
        total = total + cores[k][...].astype(jnp.float32)
    p_at = lax.broadcasted_iota(jnp.int32, (n_p, n_q), 0)
    q_at = lax.broadcasted_iota(jnp.int32, (n_p, n_q), 1)
    q_at = lax.div(q_at, col_pad) * col_width + lax.rem(q_at, col_pad)
    p_chunk, p_in = lax.div(p_at, row_pad), lax.rem(p_at, row_pad)
    p_source = lax.bitwise_xor(p_chunk, own_col[0]) if by_pairs(n_col) else p_chunk
    p_at = p_source * row_width + p_in
    keep = (p_at < row_rank[0]) & (q_at < col_rank[0])
    core = jnp.where(keep, total, 0.0).astype(jnp.bfloat16)

    old_at = lax.broadcasted_iota(jnp.int32, (rank_cap, row_count), 0)
    kept_v = jnp.where(old_at < old_rank[0, 0], base_v[...], jnp.zeros_like(base_v))
    new_at = lax.broadcasted_iota(jnp.int32, (half, row_count), 0)
    probe = sketch[0:half, :]
    probe = jnp.where(new_at < new_rank[0, 0], probe, jnp.zeros_like(probe))

    left_small = dot_nt(probe, kept_v).astype(jnp.bfloat16)
    across = dot_nt(probe, right_u[...]).astype(jnp.bfloat16)
    middle = dot_nt(across, core).astype(jnp.bfloat16)
    range_y = dot_nn(left_small, base_u[...]) - dot_nn(middle, left_u[...])
    diag_at = lax.broadcasted_iota(jnp.int32, (half, half), 0)
    diag_on = diag_at == lax.broadcasted_iota(jnp.int32, (half, half), 1)
    padding = jnp.where(diag_on & (diag_at >= new_rank[0, 0]), 1.0, 0.0)
    gram = dot_nt(range_y, range_y, FULL) + padding
    basis = dot_nn(inverse_factor(gram, min(half, round_up(rank_cap // 2, SUBLANES))), range_y, FULL)
    out_u = (jnp.sqrt(jnp.float32(row_count)) * basis).astype(jnp.bfloat16)
    back_small = dot_nt(out_u, base_u[...]).astype(jnp.bfloat16)
    side_small = dot_nt(out_u, left_u[...]).astype(jnp.bfloat16)
    turned = dot_nn(side_small, core).astype(jnp.bfloat16)
    summed = dot_nn(back_small, kept_v) - dot_nn(turned, right_u[...])
    new_u[0:half, :] = out_u
    new_v[0:half, :] = (summed / jnp.float32(row_count)).astype(jnp.bfloat16)
    if half < rank_cap:
        new_u[half:, :] = jnp.zeros((rank_cap - half, row_count), jnp.bfloat16)
        new_v[half:, :] = jnp.zeros((rank_cap - half, row_count), jnp.bfloat16)


def on_device(
    diag_inverse,
    row_u,
    row_v,
    col_u,
    col_v,
    tile_u,
    tile_v,
    sketch,
    row_rank,
    col_rank,
    old_rank,
    new_rank,
    n_row,
    n_col,
):
    own_row = jnp.reshape(lax.axis_index("row").astype(jnp.int32), (1,))
    own_col = jnp.reshape(lax.axis_index("col").astype(jnp.int32), (1,))
    row_share, row_count = diag_inverse.shape
    rank_cap = tile_u.shape[3]
    row_width, col_width = row_v.shape[2], col_v.shape[2]
    row_pad, col_pad = round_up(row_width, PACK), round_up(col_width, PACK)
    n_p, n_q = n_col * row_pad, n_row * col_pad
    half = min(round_up(rank_cap // 2, LANES), rank_cap)
    bf16 = jnp.bfloat16
    shape = jax.ShapeDtypeStruct

    row_chunks = spread(row_v[0].T, "row", n_row)
    col_chunks = spread(col_v[0].T, "row", n_row)
    right_chunks = spread(col_u[0].T, "row", n_row)
    solved = call(
        functools.partial(row_solve_body, pad=row_pad),
        shape((n_row * row_pad, row_share), bf16),
        0,
        n_row + 1,
        [pltpu.VMEM((n_row * row_pad, row_count), bf16)],
    )(*row_chunks, diag_inverse)
    solved = spread_near(solved, "col", n_col)
    left_chunks = spread_near(row_u[0].T, "col", n_col)
    parts = call(
        functools.partial(core_body, n_row=n_row, n_col=n_col, row_pad=row_pad, col_pad=col_pad),
        [shape((n_p, n_q), bf16)] * n_row,
        1,
        n_row + 1 + n_col,
        [pltpu.VMEM((n_q, row_count), bf16)],
    )(own_row, *col_chunks, diag_inverse, *solved)
    cores = hand_out(list(parts), "row", n_row)
    new_u, new_v = call(
        functools.partial(
            tile_body, n_row=n_row, n_col=n_col, row_pad=row_pad, col_pad=col_pad, half=half
        ),
        [shape((rank_cap, row_count), bf16)] * 2,
        6,
        2 * n_row + n_col + 3,
        [pltpu.VMEM((n_p, row_count), bf16), pltpu.VMEM((n_q, row_count), bf16)],
    )(
        own_col,
        own_row,
        row_rank,
        col_rank,
        old_rank,
        new_rank,
        *cores,
        *left_chunks,
        *right_chunks,
        tile_u[0, 0].T,
        tile_v[0, 0].T,
        sketch.T,
    )
    return (new_u.T[None, None], new_v.T[None, None])


def solution(mesh):
    in_specs = (
        P("row", None),
        P("row", None, "col"),
        P("row", None, "col"),
        P("col", None, "row"),
        P("col", None, "row"),
        P("row", "col", None, None),
        P("row", "col", None, None),
        P(),
        P("row"),
        P("col"),
        P("row", "col"),
        P("row", "col"),
    )
    out_specs = (P("row", "col", None, None), P("row", "col", None, None))
    body = functools.partial(on_device, n_row=mesh.shape["row"], n_col=mesh.shape["col"])
    return jax.shard_map(body, mesh=mesh, in_specs=in_specs, out_specs=out_specs, check_vma=False)
```

time: 165 us -> 60.1 us (0.36)
  blocking collectives: 66.6 us -> 0 us
  other arithmetic: 51.8 us -> 0 us
  starting transfers between devices: 0.04 us -> 27.8 us
  matrix products: 24.9 us -> 0 us
  Pallas kernels: 0 us -> 16.6 us
  between operations: 18.3 us -> 3.47 us
  waiting for transfers between devices: 0.7 us -> 10.6 us
    all_gather x4 -> x0, blocking collectives: 66.6 us -> none  [the longest x1 19.2 us: on_device(): lax.all_gather(row_v, 'col', axis=2, tiled=True)]
    another operation x13 -> x0, other arithmetic: 51.4 us -> none  [the longest x7 31.6 us: tile_update(): gram_factor = jnp.linalg.cholesky(gram)]
    ppermute x0 -> x26, starting transfers between devices: none -> 27.8 us  [swap(): return lax.ppermute(x, axis, [(i, i ^ k) for i in range(n)])]
    dot_general x9 -> x0, matrix products: 20.9 us -> none  [the longest x1 4.65 us: solve_share(): solved = jnp.dot(inverse, values, preferred_element_type=jnp.float32)]
    pallas_call x0 -> x3, Pallas kernels: none -> 16.6 us  [the longest x1 10.4 us: on_device(): call(functools.partial(tile_body, n_row=n_row, n_col=n_col, row_pad=row_p...]
    ppermute x0 -> x26, waiting for transfers between devices: none -> 10.6 us  [swap(): return lax.ppermute(x, axis, [(i, i ^ k) for i in range(n)])]
    another operation x5 -> x0, matrix products: 3.98 us -> none  [the longest x3 3.4 us: tile_update(): jax.scipy.linalg.solve_triangular(gram_factor, range_y.T, lower=True)]
  transfers between devices with their start and end apart: 1 -> 26, of which waited for: 0 -> 6; matrix products, arithmetic and copies ran while one was open for 2% -> 0% of each run, Pallas kernels for 0% -> 10%
where the time goes in v1:
time: 60.1 us; the launch traced here: 59.9 us
  starting transfers between devices  27.8 us (46%)
  Pallas kernels  16.6 us (28%)
  waiting for transfers between devices  10.6 us (18%)
  between operations  3.47 us (6%)
  local copies, waits for them, and re-layouts  1.36 us (2%)
    ppermute x26, starting transfers between devices, swap(): return lax.ppermute(x, axis, [(i, i ^ k) for i in range(n)])  27.8 us
    ppermute x26, waiting for transfers between devices, swap(): return lax.ppermute(x, axis, [(i, i ^ k) for i in range(n)])  10.6 us
    pallas_call x1, Pallas kernels, on_device(): call(functools.partial(tile_body, n_row=n_row, n_col=n_col, row_pad=row_p...  10.4 us
    pallas_call x1, Pallas kernels, on_device(): call(functools.partial(core_body, n_row=n_row, n_col=n_col, row_pad=row_p...  3.73 us
    pallas_call x1, Pallas kernels, on_device(): call(functools.partial(row_solve_body, pad=row_pad), shape((n_row * row_p...  2.47 us
    unnamed x54, local copies, waits for them, and re-layouts  1.36 us
  transfers between devices with their start and end apart: 26, of which 6 were waited for; matrix products, arithmetic and copies ran while one was open for 0% of the time, Pallas kernels for 10%

profile of v1, /device:TPU:0, one launch (start us, length us, event | category | flops | bytes accessed | tf_op | source)
XLA Modules:
  0.0 59.9 jit_solution(4327305234143037346)
XLA Ops:
  0.6 5.1 %collective-permute-start.21 = (bf16[28,1376]{1,0:T(8,128)(2,1)}, bf16[28,1376]{1,0:T(8,128)(2,1)S(1)}, u32[]{:S(2)}, u32[]{:S(2)}) collective-permute-start(bf16[28,1376]{1,0:T(8,128)(2,1)} %bitcast.42), channel_id=1, source_target_pairs={{0,6},{1,7},{2,4},{3,5},{4,2},{5,3},{6,0},{7,1},{8,14},{9,15},{10,... | collective-permute-start | bytes 231176 | tf_op jit(solution)/shard_map/ppermute | solution.py:35
  5.8 0.0 collective-permute-start.19
  5.8 0.6 %collective-permute-start.17 = (bf16[28,1376]{1,0:T(8,128)(2,1)}, bf16[28,1376]{1,0:T(8,128)(2,1)S(1)}, u32[]{:S(2)}, u32[]{:S(2)}) collective-permute-start(bf16[28,1376]{1,0:T(8,128)(2,1)} %bitcast.44), channel_id=1, source_target_pairs={{0,2},{1,3},{2,0},{3,1},{4,6},{5,7},{6,4},{7,5},{8,10},{9,11},{10,... | collective-permute-start | bytes 231176 | tf_op jit(solution)/shard_map/ppermute | solution.py:35
  6.4 2.6 %collective-permute-start.5 = (bf16[28,1376]{1,0:T(8,128)(2,1)}, bf16[28,1376]{1,0:T(8,128)(2,1)S(1)}, u32[]{:S(2)}, u32[]{:S(2)}) collective-permute-start(bf16[28,1376]{1,0:T(8,128)(2,1)} %bitcast.38), channel_id=1, source_target_pairs={{0,24},{8,16},{16,8},{24,0},{1,25},{9,17},{17,9},{25,1},{2,26},{10... | collective-permute-start | bytes 231176 | tf_op jit(solution)/shard_map/ppermute | solution.py:35
  9.0 0.5 collective-permute-start.4
  9.5 0.0 collective-permute-done.21.refs_16_
  9.5 1.4 %collective-permute-start.3 = (bf16[28,1376]{1,0:T(8,128)(2,1)}, bf16[28,1376]{1,0:T(8,128)(2,1)S(1)}, u32[]{:S(2)}, u32[]{:S(2)}) collective-permute-start(bf16[28,1376]{1,0:T(8,128)(2,1)} %bitcast.40), channel_id=1, source_target_pairs={{0,8},{8,0},{16,24},{24,16},{1,9},{9,1},{17,25},{25,17},{2,10},{10... | collective-permute-start | bytes 231176 | tf_op jit(solution)/shard_map/ppermute | solution.py:35
  10.9 2.7 %collective-permute-done.19.refs_14_ = bf16[28,1376]{1,0:T(8,128)(2,1)S(1)} collective-permute-done((bf16[28,1376]{1,0:T(8,128)(2,1)}, bf16[28,1376]{1,0:T(8,128)(2,1)S(1)}, u32[]{:S(2)}, u32[]{:S(2)}) %collective-permute-start.19) | collective-permute-done | bytes 77088 | tf_op jit(solution)/shard_map/ppermute | solution.py:35
  13.6 2.4 %collective-permute-start.2 = (bf16[56,1376]{1,0:T(8,128)(2,1)}, bf16[56,1376]{1,0:T(8,128)(2,1)S(1)}, u32[]{:S(2)}, u32[]{:S(2)}) collective-permute-start(bf16[56,1376]{1,0:T(8,128)(2,1)} %bitcast.34), channel_id=1, source_target_pairs={{0,24},{8,16},{16,8},{24,0},{1,25},{9,17},{17,9},{25,1},{2,26},{10... | collective-permute-start | bytes 462344 | tf_op jit(solution)/shard_map/ppermute | solution.py:35
  16.0 0.0 collective-permute-done.5.refs_3_
  16.0 0.6 collective-permute-start.1
  16.6 0.5 collective-permute-start
  17.2 0.1 copy-done.18
  17.2 0.5 copy-done.19
  17.8 2.5 %shard_map.131.refs_6_ = bf16[128,344]{1,0:T(8,128)(2,1)} custom-call(bf16[28,1376]{1,0:T(8,128)(2,1)} %bitcast.41, bf16[28,1376]{1,0:T(8,128)(2,1)} %copy-done.19, bf16[28,1376]{1,0:T(8,128)(2,1)} %copy-done.18, bf16[28,1376]{1,0:T(8,128)(2,1)} %copy-done.17, bf16[344,1376]{1,0:T(8,128)(2,1)} %refs_5_.2), custom_call_target="tpu_custom_call" | custom-call | tf_op jit(solution)/shard_map/pallas_call | solution.py:235
  20.3 2.7 %collective-permute-start.11 = (bf16[128,344]{1,0:T(8,128)(2,1)}, bf16[128,344]{1,0:T(8,128)(2,1)S(1)}, u32[]{:S(2)}, u32[]{:S(2)}) collective-permute-start(bf16[128,344]{1,0:T(8,128)(2,1)} %shard_map.131.refs_6_), channel_id=1, source_target_pairs={{0,6},{1,7},{2,4},{3,5},{4,2},{5,3},{6,0},{7,1},{8,14},{9,15},{10,... | collective-permute-start | bytes 264200 | tf_op jit(solution)/shard_map/ppermute | solution.py:35
  22.9 0.0 collective-permute-done.22.refs_17_
  22.9 0.3 collective-permute-start.9
  23.2 0.0 collective-permute-done.2.refs_4_
  23.2 1.5 %collective-permute-start.7 = (bf16[128,344]{1,0:T(8,128)(2,1)}, bf16[128,344]{1,0:T(8,128)(2,1)S(1)}, u32[]{:S(2)}, u32[]{:S(2)}) collective-permute-start(bf16[128,344]{1,0:T(8,128)(2,1)} %shard_map.131.refs_6_), channel_id=1, source_target_pairs={{0,2},{1,3},{2,0},{3,1},{4,6},{5,7},{6,4},{7,5},{8,10},{9,11},{10,... | collective-permute-start | bytes 264200 | tf_op jit(solution)/shard_map/ppermute | solution.py:35
  24.7 0.0 collective-permute-done.1.refs_3_
  24.7 3.3 %collective-permute-done.11.refs_12_ = bf16[128,344]{1,0:T(8,128)(2,1)S(1)} collective-permute-done((bf16[128,344]{1,0:T(8,128)(2,1)}, bf16[128,344]{1,0:T(8,128)(2,1)S(1)}, u32[]{:S(2)}, u32[]{:S(2)}) %collective-permute-start.11) | collective-permute-done | bytes 88096 | tf_op jit(solution)/shard_map/ppermute | solution.py:35
  28.1 0.0 collective-permute-start.12
  28.1 0.0 collective-permute-done.refs_2_
  28.1 0.0 copy-start.6
  28.1 2.5 %collective-permute-start.25 = (bf16[56,1376]{1,0:T(8,128)(2,1)S(1)}, bf16[56,1376]{1,0:T(8,128)(2,1)S(1)}, u32[]{:S(2)}, u32[]{:S(2)}) collective-permute-start(bf16[56,1376]{1,0:T(8,128)(2,1)S(1)} %bitcast.31), channel_id=1, source_target_pairs={{0,24},{8,16},{16,8},{24,0},{1,25},{9,17},{17,9},{25,1},{2,26},{10... | collective-permute-start | bytes 462344 | tf_op jit(solution)/shard_map/ppermute | solution.py:35
  30.6 1.7 %collective-permute-done.9.refs_10_ = bf16[128,344]{1,0:T(8,128)(2,1)S(1)} collective-permute-done((bf16[128,344]{1,0:T(8,128)(2,1)}, bf16[128,344]{1,0:T(8,128)(2,1)S(1)}, u32[]{:S(2)}, u32[]{:S(2)}) %collective-permute-start.9) | collective-permute-done | bytes 88096 | tf_op jit(solution)/shard_map/ppermute | solution.py:35
  32.3 0.0 collective-permute-start.10
  32.3 0.0 collective-permute-done.7.refs_8_
  32.3 0.5 collective-permute-start.8
  32.8 0.0 collective-permute-done.6.refs_7_
  32.8 0.1 collective-permute-start.20
  33.0 0.5 collective-permute-start.18
  33.5 0.1 collective-permute-done.10.refs_11_
  33.6 1.2 %collective-permute-start.24 = (bf16[56,1376]{1,0:T(8,128)(2,1)S(1)}, bf16[56,1376]{1,0:T(8,128)(2,1)S(1)}, u32[]{:S(2)}, u32[]{:S(2)}) collective-permute-start(bf16[56,1376]{1,0:T(8,128)(2,1)S(1)} %bitcast.32), channel_id=1, source_target_pairs={{0,16},{8,24},{16,0},{24,8},{1,17},{9,25},{17,1},{25,9},{2,18},{10... | collective-permute-start | bytes 462344 | tf_op jit(solution)/shard_map/ppermute | solution.py:35
  34.8 1.1 %collective-permute-start.23 = (bf16[56,1376]{1,0:T(8,128)(2,1)S(1)}, bf16[56,1376]{1,0:T(8,128)(2,1)S(1)}, u32[]{:S(2)}, u32[]{:S(2)}) collective-permute-start(bf16[56,1376]{1,0:T(8,128)(2,1)S(1)} %bitcast.33), channel_id=1, source_target_pairs={{0,8},{8,0},{16,24},{24,16},{1,9},{9,1},{17,25},{25,17},{2,10},{10... | collective-permute-start | bytes 462344 | tf_op jit(solution)/shard_map/ppermute | solution.py:35
  36.0 3.7 %shard_map.132 = (bf16[256,256]{1,0:T(8,128)(2,1)}, bf16[256,256]{1,0:T(8,128)(2,1)}, bf16[256,256]{1,0:T(8,128)(2,1)}, bf16[256,256]{1,0:T(8,128)(2,1)}) custom-call(s32[1]{0:T(128)} %bitcast.1.refs_0_.refs_1_, bf16[56,1376]{1,0:T(8,128)(2,1)} %bitcast.37, bf16[56,1376]{1,0:T(8,128)(2,1)} %copy-done.6, bf16[56,1376]{1,0:T(8,128)(2,1)} %copy-done.5, ...), custom_call_target="tpu_custom_call" | custom-call | tf_op jit(solution)/shard_map/pallas_call | solution.py:244
  39.8 0.0 collective-permute-done.20.refs_15_
  39.8 1.0 %collective-permute-start.13 = (bf16[256,256]{1,0:T(8,128)(2,1)}, bf16[256,256]{1,0:T(8,128)(2,1)S(1)}, u32[]{:S(2)}, u32[]{:S(2)}) collective-permute-start(bf16[256,256]{1,0:T(8,128)(2,1)} %get-tuple-element.9), channel_id=1, source_target_pairs={{0,8},{8,0},{16,24},{24,16},{1,9},{9,1},{17,25},{25,17},{2,10},{10... | collective-permute-start | bytes 393224 | tf_op jit(solution)/shard_map/ppermute | solution.py:35
  40.8 0.8 %collective-permute-start.14 = (bf16[256,256]{1,0:T(8,128)(2,1)}, bf16[256,256]{1,0:T(8,128)(2,1)S(1)}, u32[]{:S(2)}, u32[]{:S(2)}) collective-permute-start(bf16[256,256]{1,0:T(8,128)(2,1)} %get-tuple-element.10), channel_id=1, source_target_pairs={{0,16},{8,24},{16,0},{24,8},{1,17},{9,25},{17,1},{25,9},{2,18},{10... | collective-permute-start | bytes 393224 | tf_op jit(solution)/shard_map/ppermute | solution.py:35
  41.6 0.0 collective-permute-done.25.refs_21_
  41.6 1.8 %collective-permute-start.15 = (bf16[256,256]{1,0:T(8,128)(2,1)}, bf16[256,256]{1,0:T(8,128)(2,1)S(1)}, u32[]{:S(2)}, u32[]{:S(2)}) collective-permute-start(bf16[256,256]{1,0:T(8,128)(2,1)} %get-tuple-element.11), channel_id=1, source_target_pairs={{0,24},{8,16},{16,8},{24,0},{1,25},{9,17},{17,9},{25,1},{2,26},{10... | collective-permute-start | bytes 393224 | tf_op jit(solution)/shard_map/ppermute | solution.py:35
  45.9 0.0 collective-permute-done.24.refs_20_
  46.0 0.1 collective-permute-done.13.refs_7_
  46.1 2.7 %collective-permute-done.14.refs_8_ = bf16[256,256]{1,0:T(8,128)(2,1)S(1)} collective-permute-done((bf16[256,256]{1,0:T(8,128)(2,1)}, bf16[256,256]{1,0:T(8,128)(2,1)S(1)}, u32[]{:S(2)}, u32[]{:S(2)}) %collective-permute-start.14) | collective-permute-done | bytes 131104 | tf_op jit(solution)/shard_map/ppermute | solution.py:35
  48.8 0.6 copy-done.8
  49.4 0.1 copy-done.9
  49.4 10.4 %shard_map.133 = (bf16[224,1376]{1,0:T(8,128)(2,1)}, bf16[224,1376]{1,0:T(8,128)(2,1)}) custom-call(s32[1]{0:T(128)} %bitcast.refs_0_, s32[1]{0:T(128)} %bitcast.1.refs_0_.refs_1_, s32[1]{0:T(128)S(6)} %copy.14.refs_2_, s32[1]{0:T(128)S(6)} %copy.15.refs_3_, s32[1,1]{1,0:T(1,128)S(6)} %copy.16.refs_4_, s32[1,1]{1,0:T(1,128)S(6)} %copy.17.refs_5_, ...), custom_call_target="tpu_custom_call" | custom-call | tf_op jit(solution)/shard_map/pallas_call | solution.py:252
  (61 shorter events, 0.1 us)
Async XLA Ops:
  0.6 8.9 %collective-permute-start.21 = (bf16[28,1376]{1,0:T(8,128)(2,1)}, bf16[28,1376]{1,0:T(8,128)(2,1)S(1)}, u32[]{:S(2)}, u32[]{:S(2)}) collective-permute-start(bf16[28,1376]{1,0:T(8,128)(2,1)} %bitcast.42), channel_id=1, source_target_pairs={{0,6},{1,7},{2,4},{3,5},{4,2},{5,3},{6,0},{7,1},{8,14},{9,15},{10,... | collective-permute-start | bytes 231176 | tf_op jit(solution)/shard_map/ppermute | solution.py:35
  5.8 7.8 %collective-permute-start.19 = (bf16[28,1376]{1,0:T(8,128)(2,1)}, bf16[28,1376]{1,0:T(8,128)(2,1)S(1)}, u32[]{:S(2)}, u32[]{:S(2)}) collective-permute-start(bf16[28,1376]{1,0:T(8,128)(2,1)} %bitcast.43), channel_id=1, source_target_pairs={{0,4},{1,5},{2,6},{3,7},{4,0},{5,1},{6,2},{7,3},{8,12},{9,13},{10,... | collective-permute-start | bytes 231176 | tf_op jit(solution)/shard_map/ppermute | solution.py:35
  5.8 10.2 %collective-permute-start.17 = (bf16[28,1376]{1,0:T(8,128)(2,1)}, bf16[28,1376]{1,0:T(8,128)(2,1)S(1)}, u32[]{:S(2)}, u32[]{:S(2)}) collective-permute-start(bf16[28,1376]{1,0:T(8,128)(2,1)} %bitcast.44), channel_id=1, source_target_pairs={{0,2},{1,3},{2,0},{3,1},{4,6},{5,7},{6,4},{7,5},{8,10},{9,11},{10,... | collective-permute-start | bytes 231176 | tf_op jit(solution)/shard_map/ppermute | solution.py:35
  6.4 9.6 %collective-permute-start.5 = (bf16[28,1376]{1,0:T(8,128)(2,1)}, bf16[28,1376]{1,0:T(8,128)(2,1)S(1)}, u32[]{:S(2)}, u32[]{:S(2)}) collective-permute-start(bf16[28,1376]{1,0:T(8,128)(2,1)} %bitcast.38), channel_id=1, source_target_pairs={{0,24},{8,16},{16,8},{24,0},{1,25},{9,17},{17,9},{25,1},{2,26},{10... | collective-permute-start | bytes 231176 | tf_op jit(solution)/shard_map/ppermute | solution.py:35
  9.0 7.6 %collective-permute-start.4 = (bf16[28,1376]{1,0:T(8,128)(2,1)}, bf16[28,1376]{1,0:T(8,128)(2,1)S(1)}, u32[]{:S(2)}, u32[]{:S(2)}) collective-permute-start(bf16[28,1376]{1,0:T(8,128)(2,1)} %bitcast.39), channel_id=1, source_target_pairs={{0,16},{8,24},{16,0},{24,8},{1,17},{9,25},{17,1},{25,9},{2,18},{10... | collective-permute-start | bytes 231176 | tf_op jit(solution)/shard_map/ppermute | solution.py:35
  9.5 10.7 %copy-start.20 = (bf16[28,1376]{1,0:T(8,128)(2,1)}, bf16[28,1376]{1,0:T(8,128)(2,1)S(1)}, u32[]{:S(2)}) copy-start(bf16[28,1376]{1,0:T(8,128)(2,1)S(1)} %collective-permute-done.21.refs_16_) | copy-start | bytes 231172
  9.5 7.6 %collective-permute-start.3 = (bf16[28,1376]{1,0:T(8,128)(2,1)}, bf16[28,1376]{1,0:T(8,128)(2,1)S(1)}, u32[]{:S(2)}, u32[]{:S(2)}) collective-permute-start(bf16[28,1376]{1,0:T(8,128)(2,1)} %bitcast.40), channel_id=1, source_target_pairs={{0,8},{8,0},{16,24},{24,16},{1,9},{9,1},{17,25},{25,17},{2,10},{10... | collective-permute-start | bytes 231176 | tf_op jit(solution)/shard_map/ppermute | solution.py:35
  13.5 19.3 %copy-start.21 = (bf16[28,1376]{1,0:T(8,128)(2,1)}, bf16[28,1376]{1,0:T(8,128)(2,1)S(1)}, u32[]{:S(2)}) copy-start(bf16[28,1376]{1,0:T(8,128)(2,1)S(1)} %collective-permute-done.19.refs_14_) | copy-start | bytes 231172
  13.5 14.5 %copy-start = (bf16[1,1376,56]{1,2,0:T(8,128)(2,1)S(1)}, bf16[1,1376,56]{1,2,0:T(8,128)(2,1)}, u32[]{:S(2)}) copy-start(bf16[1,1376,56]{1,2,0:T(8,128)(2,1)} %param.15) | copy-start | bytes 462340
  13.6 9.7 %collective-permute-start.2 = (bf16[56,1376]{1,0:T(8,128)(2,1)}, bf16[56,1376]{1,0:T(8,128)(2,1)S(1)}, u32[]{:S(2)}, u32[]{:S(2)}) collective-permute-start(bf16[56,1376]{1,0:T(8,128)(2,1)} %bitcast.34), channel_id=1, source_target_pairs={{0,24},{8,16},{16,8},{24,0},{1,25},{9,17},{17,9},{25,1},{2,26},{10... | collective-permute-start | bytes 462344 | tf_op jit(solution)/shard_map/ppermute | solution.py:35
  16.0 17.0 %copy-start.22 = (bf16[28,1376]{1,0:T(8,128)(2,1)}, bf16[28,1376]{1,0:T(8,128)(2,1)S(1)}, u32[]{:S(2)}) copy-start(bf16[28,1376]{1,0:T(8,128)(2,1)S(1)} %collective-permute-done.17.refs_12_) | copy-start | bytes 231172
  16.0 4.3 %collective-permute-start.16 = (bf16[28,1376]{1,0:T(8,128)(2,1)}, bf16[28,1376]{1,0:T(8,128)(2,1)S(1)}, u32[]{:S(2)}, u32[]{:S(2)}) collective-permute-start(bf16[28,1376]{1,0:T(8,128)(2,1)} %bitcast.45), channel_id=1, source_target_pairs={{0,1},{1,0},{2,3},{3,2},{4,5},{5,4},{6,7},{7,6},{8,9},{9,8},{10,11... | collective-permute-start | bytes 231176 | tf_op jit(solution)/shard_map/ppermute | solution.py:35
  16.0 8.7 %collective-permute-start.1 = (bf16[56,1376]{1,0:T(8,128)(2,1)}, bf16[56,1376]{1,0:T(8,128)(2,1)S(1)}, u32[]{:S(2)}, u32[]{:S(2)}) collective-permute-start(bf16[56,1376]{1,0:T(8,128)(2,1)} %bitcast.35), channel_id=1, source_target_pairs={{0,16},{8,24},{16,0},{24,8},{1,17},{9,25},{17,1},{25,9},{2,18},{10... | collective-permute-start | bytes 462344 | tf_op jit(solution)/shard_map/ppermute | solution.py:35
  16.6 11.5 %collective-permute-start = (bf16[56,1376]{1,0:T(8,128)(2,1)}, bf16[56,1376]{1,0:T(8,128)(2,1)S(1)}, u32[]{:S(2)}, u32[]{:S(2)}) collective-permute-start(bf16[56,1376]{1,0:T(8,128)(2,1)} %bitcast.36), channel_id=1, source_target_pairs={{0,8},{8,0},{16,24},{24,16},{1,9},{9,1},{17,25},{25,17},{2,10},{10... | collective-permute-start | bytes 462344 | tf_op jit(solution)/shard_map/ppermute | solution.py:35
  17.1 5.8 %collective-permute-start.22 = (bf16[28,1376]{1,0:T(8,128)(2,1)S(1)}, bf16[28,1376]{1,0:T(8,128)(2,1)S(1)}, u32[]{:S(2)}, u32[]{:S(2)}) collective-permute-start(bf16[28,1376]{1,0:T(8,128)(2,1)S(1)} %collective-permute-done.21.refs_16_), channel_id=1, source_target_pairs={{0,1},{1,0},{2,3},{3,2},{4,5},{5,4},{6,7},{7,6},{8,9},{9,8},{10,11... | collective-permute-start | bytes 231176 | tf_op jit(solution)/shard_map/ppermute | solution.py:35
  20.3 19.5 %copy-start.23 = (bf16[28,1376]{1,0:T(8,128)(2,1)}, bf16[28,1376]{1,0:T(8,128)(2,1)S(1)}, u32[]{:S(2)}) copy-start(bf16[28,1376]{1,0:T(8,128)(2,1)S(1)} %collective-permute-done.16.refs_11_) | copy-start | bytes 231172
  20.3 7.8 %collective-permute-start.11 = (bf16[128,344]{1,0:T(8,128)(2,1)}, bf16[128,344]{1,0:T(8,128)(2,1)S(1)}, u32[]{:S(2)}, u32[]{:S(2)}) collective-permute-start(bf16[128,344]{1,0:T(8,128)(2,1)} %shard_map.131.refs_6_), channel_id=1, source_target_pairs={{0,6},{1,7},{2,4},{3,5},{4,2},{5,3},{6,0},{7,1},{8,14},{9,15},{10,... | collective-permute-start | bytes 264200 | tf_op jit(solution)/shard_map/ppermute | solution.py:35
  22.9 16.8 %copy-start.24 = (bf16[28,1376]{1,0:T(8,128)(2,1)}, bf16[28,1376]{1,0:T(8,128)(2,1)S(1)}, u32[]{:S(2)}) copy-start(bf16[28,1376]{1,0:T(8,128)(2,1)S(1)} %collective-permute-done.22.refs_17_) | copy-start | bytes 231172
  22.9 9.4 %collective-permute-start.9 = (bf16[128,344]{1,0:T(8,128)(2,1)}, bf16[128,344]{1,0:T(8,128)(2,1)S(1)}, u32[]{:S(2)}, u32[]{:S(2)}) collective-permute-start(bf16[128,344]{1,0:T(8,128)(2,1)} %shard_map.131.refs_6_), channel_id=1, source_target_pairs={{0,4},{1,5},{2,6},{3,7},{4,0},{5,1},{6,2},{7,3},{8,12},{9,13},{10,... | collective-permute-start | bytes 264200 | tf_op jit(solution)/shard_map/ppermute | solution.py:35
  23.2 12.7 %copy-start.4 = (bf16[56,1376]{1,0:T(8,128)(2,1)}, bf16[56,1376]{1,0:T(8,128)(2,1)S(1)}, u32[]{:S(2)}) copy-start(bf16[56,1376]{1,0:T(8,128)(2,1)S(1)} %collective-permute-done.2.refs_4_) | copy-start | bytes 462340
  23.2 9.1 %collective-permute-start.7 = (bf16[128,344]{1,0:T(8,128)(2,1)}, bf16[128,344]{1,0:T(8,128)(2,1)S(1)}, u32[]{:S(2)}, u32[]{:S(2)}) collective-permute-start(bf16[128,344]{1,0:T(8,128)(2,1)} %shard_map.131.refs_6_), channel_id=1, source_target_pairs={{0,2},{1,3},{2,0},{3,1},{4,6},{5,7},{6,4},{7,5},{8,10},{9,11},{10,... | collective-permute-start | bytes 264200 | tf_op jit(solution)/shard_map/ppermute | solution.py:35
  24.7 11.2 %copy-start.5 = (bf16[56,1376]{1,0:T(8,128)(2,1)}, bf16[56,1376]{1,0:T(8,128)(2,1)S(1)}, u32[]{:S(2)}) copy-start(bf16[56,1376]{1,0:T(8,128)(2,1)S(1)} %collective-permute-done.1.refs_3_) | copy-start | bytes 462340
  24.7 8.1 %collective-permute-start.6 = (bf16[128,344]{1,0:T(8,128)(2,1)}, bf16[128,344]{1,0:T(8,128)(2,1)S(1)}, u32[]{:S(2)}, u32[]{:S(2)}) collective-permute-start(bf16[128,344]{1,0:T(8,128)(2,1)} %shard_map.131.refs_6_), channel_id=1, source_target_pairs={{0,1},{1,0},{2,3},{3,2},{4,5},{5,4},{6,7},{7,6},{8,9},{9,8},{10,11... | collective-permute-start | bytes 264200 | tf_op jit(solution)/shard_map/ppermute | solution.py:35
  28.1 7.9 %copy-start.10 = (bf16[128,344]{1,0:T(8,128)(2,1)}, bf16[128,344]{1,0:T(8,128)(2,1)S(1)}, u32[]{:S(2)}) copy-start(bf16[128,344]{1,0:T(8,128)(2,1)S(1)} %collective-permute-done.11.refs_12_) | copy-start | bytes 264196
  28.1 4.9 %collective-permute-start.12 = (bf16[128,344]{1,0:T(8,128)(2,1)S(1)}, bf16[128,344]{1,0:T(8,128)(2,1)S(1)}, u32[]{:S(2)}, u32[]{:S(2)}) collective-permute-start(bf16[128,344]{1,0:T(8,128)(2,1)S(1)} %collective-permute-done.11.refs_12_), channel_id=1, source_target_pairs={{0,1},{1,0},{2,3},{3,2},{4,5},{5,4},{6,7},{7,6},{8,9},{9,8},{10,11... | collective-permute-start | bytes 264200 | tf_op jit(solution)/shard_map/ppermute | solution.py:35
  28.1 7.9 %copy-start.6 = (bf16[56,1376]{1,0:T(8,128)(2,1)}, bf16[56,1376]{1,0:T(8,128)(2,1)S(1)}, u32[]{:S(2)}) copy-start(bf16[56,1376]{1,0:T(8,128)(2,1)S(1)} %collective-permute-done.refs_2_) | copy-start | bytes 462340
  28.1 13.5 %collective-permute-start.25 = (bf16[56,1376]{1,0:T(8,128)(2,1)S(1)}, bf16[56,1376]{1,0:T(8,128)(2,1)S(1)}, u32[]{:S(2)}, u32[]{:S(2)}) collective-permute-start(bf16[56,1376]{1,0:T(8,128)(2,1)S(1)} %bitcast.31), channel_id=1, source_target_pairs={{0,24},{8,16},{16,8},{24,0},{1,25},{9,17},{17,9},{25,1},{2,26},{10... | collective-permute-start | bytes 462344 | tf_op jit(solution)/shard_map/ppermute | solution.py:35
  32.3 3.7 %copy-start.11 = (bf16[128,344]{1,0:T(8,128)(2,1)}, bf16[128,344]{1,0:T(8,128)(2,1)S(1)}, u32[]{:S(2)}) copy-start(bf16[128,344]{1,0:T(8,128)(2,1)S(1)} %collective-permute-done.9.refs_10_) | copy-start | bytes 264196
  32.3 1.3 %collective-permute-start.10 = (bf16[128,344]{1,0:T(8,128)(2,1)S(1)}, bf16[128,344]{1,0:T(8,128)(2,1)S(1)}, u32[]{:S(2)}, u32[]{:S(2)}) collective-permute-start(bf16[128,344]{1,0:T(8,128)(2,1)S(1)} %collective-permute-done.9.refs_10_), channel_id=1, source_target_pairs={{0,1},{1,0},{2,3},{3,2},{4,5},{5,4},{6,7},{7,6},{8,9},{9,8},{10,11... | collective-permute-start | bytes 264200 | tf_op jit(solution)/shard_map/ppermute | solution.py:35
  32.3 3.7 %copy-start.12 = (bf16[128,344]{1,0:T(8,128)(2,1)}, bf16[128,344]{1,0:T(8,128)(2,1)S(1)}, u32[]{:S(2)}) copy-start(bf16[128,344]{1,0:T(8,128)(2,1)S(1)} %collective-permute-done.7.refs_8_) | copy-start | bytes 264196
  32.3 2.5 %collective-permute-start.8 = (bf16[128,344]{1,0:T(8,128)(2,1)S(1)}, bf16[128,344]{1,0:T(8,128)(2,1)S(1)}, u32[]{:S(2)}, u32[]{:S(2)}) collective-permute-start(bf16[128,344]{1,0:T(8,128)(2,1)S(1)} %collective-permute-done.7.refs_8_), channel_id=1, source_target_pairs={{0,1},{1,0},{2,3},{3,2},{4,5},{5,4},{6,7},{7,6},{8,9},{9,8},{10,11... | collective-permute-start | bytes 264200 | tf_op jit(solution)/shard_map/ppermute | solution.py:35
  32.8 3.2 %copy-start.13 = (bf16[128,344]{1,0:T(8,128)(2,1)}, bf16[128,344]{1,0:T(8,128)(2,1)S(1)}, u32[]{:S(2)}) copy-start(bf16[128,344]{1,0:T(8,128)(2,1)S(1)} %collective-permute-done.6.refs_7_) | copy-start | bytes 264196
  32.8 6.9 %collective-permute-start.20 = (bf16[28,1376]{1,0:T(8,128)(2,1)S(1)}, bf16[28,1376]{1,0:T(8,128)(2,1)S(1)}, u32[]{:S(2)}, u32[]{:S(2)}) collective-permute-start(bf16[28,1376]{1,0:T(8,128)(2,1)S(1)} %collective-permute-done.19.refs_14_), channel_id=1, source_target_pairs={{0,1},{1,0},{2,3},{3,2},{4,5},{5,4},{6,7},{7,6},{8,9},{9,8},{10,11... | collective-permute-start | bytes 231176 | tf_op jit(solution)/shard_map/ppermute | solution.py:35
  33.0 3.0 %copy-start.14 = (bf16[128,344]{1,0:T(8,128)(2,1)}, bf16[128,344]{1,0:T(8,128)(2,1)S(1)}, u32[]{:S(2)}) copy-start(bf16[128,344]{1,0:T(8,128)(2,1)S(1)} %collective-permute-done.12.refs_13_) | copy-start | bytes 264196
  33.0 7.8 %collective-permute-start.18 = (bf16[28,1376]{1,0:T(8,128)(2,1)S(1)}, bf16[28,1376]{1,0:T(8,128)(2,1)S(1)}, u32[]{:S(2)}, u32[]{:S(2)}) collective-permute-start(bf16[28,1376]{1,0:T(8,128)(2,1)S(1)} %collective-permute-done.17.refs_12_), channel_id=1, source_target_pairs={{0,1},{1,0},{2,3},{3,2},{4,5},{5,4},{6,7},{7,6},{8,9},{9,8},{10,11... | collective-permute-start | bytes 231176 | tf_op jit(solution)/shard_map/ppermute | solution.py:35
  33.6 2.4 %copy-start.15 = (bf16[128,344]{1,0:T(8,128)(2,1)}, bf16[128,344]{1,0:T(8,128)(2,1)S(1)}, u32[]{:S(2)}) copy-start(bf16[128,344]{1,0:T(8,128)(2,1)S(1)} %collective-permute-done.10.refs_11_) | copy-start | bytes 264196
  33.6 12.3 %collective-permute-start.24 = (bf16[56,1376]{1,0:T(8,128)(2,1)S(1)}, bf16[56,1376]{1,0:T(8,128)(2,1)S(1)}, u32[]{:S(2)}, u32[]{:S(2)}) collective-permute-start(bf16[56,1376]{1,0:T(8,128)(2,1)S(1)} %bitcast.32), channel_id=1, source_target_pairs={{0,16},{8,24},{16,0},{24,8},{1,17},{9,25},{17,1},{25,9},{2,18},{10... | collective-permute-start | bytes 462344 | tf_op jit(solution)/shard_map/ppermute | solution.py:35
  34.8 1.2 %copy-start.16 = (bf16[128,344]{1,0:T(8,128)(2,1)}, bf16[128,344]{1,0:T(8,128)(2,1)S(1)}, u32[]{:S(2)}) copy-start(bf16[128,344]{1,0:T(8,128)(2,1)S(1)} %collective-permute-done.8.refs_9_) | copy-start | bytes 264196
  34.8 11.1 %collective-permute-start.23 = (bf16[56,1376]{1,0:T(8,128)(2,1)S(1)}, bf16[56,1376]{1,0:T(8,128)(2,1)S(1)}, u32[]{:S(2)}, u32[]{:S(2)}) collective-permute-start(bf16[56,1376]{1,0:T(8,128)(2,1)S(1)} %bitcast.33), channel_id=1, source_target_pairs={{0,8},{8,0},{16,24},{24,16},{1,9},{9,1},{17,25},{25,17},{2,10},{10... | collective-permute-start | bytes 462344 | tf_op jit(solution)/shard_map/ppermute | solution.py:35
  39.8 8.9 %copy-start.25 = (bf16[28,1376]{1,0:T(8,128)(2,1)}, bf16[28,1376]{1,0:T(8,128)(2,1)S(1)}, u32[]{:S(2)}) copy-start(bf16[28,1376]{1,0:T(8,128)(2,1)S(1)} %collective-permute-done.20.refs_15_) | copy-start | bytes 231172
  39.8 6.3 %collective-permute-start.13 = (bf16[256,256]{1,0:T(8,128)(2,1)}, bf16[256,256]{1,0:T(8,128)(2,1)S(1)}, u32[]{:S(2)}, u32[]{:S(2)}) collective-permute-start(bf16[256,256]{1,0:T(8,128)(2,1)} %get-tuple-element.9), channel_id=1, source_target_pairs={{0,8},{8,0},{16,24},{24,16},{1,9},{9,1},{17,25},{25,17},{2,10},{10... | collective-permute-start | bytes 393224 | tf_op jit(solution)/shard_map/ppermute | solution.py:35
  40.8 8.0 %copy-start.26 = (bf16[28,1376]{1,0:T(8,128)(2,1)}, bf16[28,1376]{1,0:T(8,128)(2,1)S(1)}, u32[]{:S(2)}) copy-start(bf16[28,1376]{1,0:T(8,128)(2,1)S(1)} %collective-permute-done.18.refs_13_) | copy-start | bytes 231172
  40.8 8.0 %collective-permute-start.14 = (bf16[256,256]{1,0:T(8,128)(2,1)}, bf16[256,256]{1,0:T(8,128)(2,1)S(1)}, u32[]{:S(2)}, u32[]{:S(2)}) collective-permute-start(bf16[256,256]{1,0:T(8,128)(2,1)} %get-tuple-element.10), channel_id=1, source_target_pairs={{0,16},{8,24},{16,0},{24,8},{1,17},{9,25},{17,1},{25,9},{2,18},{10... | collective-permute-start | bytes 393224 | tf_op jit(solution)/shard_map/ppermute | solution.py:35
  41.6 7.2 %copy-start.1 = (bf16[56,1376]{1,0:T(8,128)(2,1)}, bf16[56,1376]{1,0:T(8,128)(2,1)S(1)}, u32[]{:S(2)}) copy-start(bf16[56,1376]{1,0:T(8,128)(2,1)S(1)} %collective-permute-done.25.refs_21_) | copy-start | bytes 462340
  41.6 7.1 %collective-permute-start.15 = (bf16[256,256]{1,0:T(8,128)(2,1)}, bf16[256,256]{1,0:T(8,128)(2,1)S(1)}, u32[]{:S(2)}, u32[]{:S(2)}) collective-permute-start(bf16[256,256]{1,0:T(8,128)(2,1)} %get-tuple-element.11), channel_id=1, source_target_pairs={{0,24},{8,16},{16,8},{24,0},{1,25},{9,17},{17,9},{25,1},{2,26},{10... | collective-permute-start | bytes 393224 | tf_op jit(solution)/shard_map/ppermute | solution.py:35
  46.0 2.8 %copy-start.2 = (bf16[56,1376]{1,0:T(8,128)(2,1)}, bf16[56,1376]{1,0:T(8,128)(2,1)S(1)}, u32[]{:S(2)}) copy-start(bf16[56,1376]{1,0:T(8,128)(2,1)S(1)} %collective-permute-done.24.refs_20_) | copy-start | bytes 462340
  46.0 2.8 %copy-start.3 = (bf16[56,1376]{1,0:T(8,128)(2,1)}, bf16[56,1376]{1,0:T(8,128)(2,1)S(1)}, u32[]{:S(2)}) copy-start(bf16[56,1376]{1,0:T(8,128)(2,1)S(1)} %collective-permute-done.23.refs_19_) | copy-start | bytes 462340
  46.1 2.7 %copy-start.7 = (bf16[256,256]{1,0:T(8,128)(2,1)}, bf16[256,256]{1,0:T(8,128)(2,1)S(1)}, u32[]{:S(2)}) copy-start(bf16[256,256]{1,0:T(8,128)(2,1)S(1)} %collective-permute-done.13.refs_7_) | copy-start | bytes 393220
  (5 other events, 3.8 us)

commit v2 on v1

--- a/solution.py
+++ b/solution.py
@@ -6,6 +6,7 @@
 from jax.experimental import pallas as pl
 from jax.experimental.pallas import tpu as pltpu
 from jax.sharding import PartitionSpec as P
+
 
 FULL = lax.Precision.HIGHEST
 NT = (((1,), (1,)), ((), ()))
@@ -65,15 +66,17 @@
     return own ^ k if by_pairs(n) else k
 
 
-def call(body, out_shape, n_smem, n_vmem, scratch=()):
+def call(body, out_shape, smem, vmem, scratch=(), small=True):
+    outs = [jax.ShapeDtypeStruct(dims, dtype) for dims, dtype in out_shape]
     return pl.pallas_call(
         body,
-        out_shape=out_shape,
-        in_specs=[pl.BlockSpec(memory_space=pltpu.SMEM)] * n_smem
-        + [pl.BlockSpec(memory_space=pltpu.VMEM)] * n_vmem,
+        out_shape=outs,
+        in_specs=[pl.BlockSpec(memory_space=pltpu.SMEM)] * len(smem)
+        + [pl.BlockSpec(memory_space=pltpu.VMEM)] * len(vmem),
+        out_specs=[pl.BlockSpec(memory_space=pltpu.VMEM)] * len(outs),
         scratch_shapes=list(scratch),
-        compiler_params=pltpu.CompilerParams(vmem_limit_bytes=56 * 1024 * 1024),
-    )
+        compiler_params=pltpu.CompilerParams(vmem_limit_bytes=(12 if small else 56) * 2**20),
+    )(*smem, *vmem)
 
 
 def row_solve_body(*refs, pad):
@@ -86,16 +89,16 @@
 
 
 def core_body(*refs, n_row, n_col, row_pad, col_pad):
-    own, refs = refs[0], refs[1:]
+    own_row = lax.axis_index("row")
     col_chunks, refs = refs[:n_row], refs[n_row:]
     inverse, refs = refs[0], refs[1:]
     solved, refs = refs[:n_col], refs[n_col:]
     outs, stacked = refs[:n_row], refs[n_row]
     stacked[...] = jnp.zeros_like(stacked)
-    width = col_chunks[0].shape[0]
+    width = col_chunks[0].shape[0] // 2
     for k, chunk in enumerate(col_chunks):
-        at = source_of(own[0], k, n_row)
-        stacked[pl.ds(pl.multiple_of(at * col_pad, col_pad), width), :] = chunk[...]
+        at = source_of(own_row, k, n_row)
+        stacked[pl.ds(pl.multiple_of(at * col_pad, col_pad), width), :] = chunk[0:width, :]
     col_solved = dot_nt(stacked[...], inverse[...]).astype(jnp.bfloat16)
     for m in range(n_col):
         part = dot_nt(solved[m][...], col_solved).astype(jnp.bfloat16)
@@ -145,24 +148,39 @@
     return jnp.concatenate(right, axis=0)
 
 
-def tile_body(*refs, n_row, n_col, row_pad, col_pad, half):
-    (own_col, own_row, row_rank, col_rank, old_rank, new_rank), refs = refs[:6], refs[6:]
+def base_body(*refs, n_row, col_pad, half):
+    old_rank, new_rank, *refs = refs
+    own_row = lax.axis_index("row")
+    col_chunks, refs = refs[:n_row], refs[n_row:]
+    base_u, base_v, sketch, right_u, across, base_y = refs
+    rank_cap, row_count = base_u.shape
+    width = col_chunks[0].shape[0] // 2
+    right_u[...] = jnp.zeros_like(right_u)
+    for k, chunk in enumerate(col_chunks):
+        at = source_of(own_row, k, n_row)
+        right_u[pl.ds(pl.multiple_of(at * col_pad, col_pad), width), :] = chunk[width : 2 * width, :]
+    old_at = lax.broadcasted_iota(jnp.int32, (rank_cap, row_count), 0)
+    kept_v = jnp.where(old_at < old_rank[0, 0], base_v[...], jnp.zeros_like(base_v))
+    new_at = lax.broadcasted_iota(jnp.int32, (half, row_count), 0)
+    probe = sketch[0:half, :]
+    probe = jnp.where(new_at < new_rank[0, 0], probe, jnp.zeros_like(probe))
+    left_small = dot_nt(probe, kept_v).astype(jnp.bfloat16)
+    across[...] = dot_nt(probe, right_u[...]).astype(jnp.bfloat16)
+    base_y[...] = dot_nn(left_small, base_u[...])
+
+
+def tile_body(*refs, n_row, n_col, row_pad, col_pad, row_width, col_width, half):
+    (row_rank, col_rank, old_rank, new_rank), refs = refs[:4], refs[4:]
+    own_col = lax.axis_index("col")
     cores, refs = refs[:n_row], refs[n_row:]
     row_chunks, refs = refs[:n_col], refs[n_col:]
-    col_chunks, refs = refs[:n_row], refs[n_row:]
-    base_u, base_v, sketch, new_u, new_v, left_u, right_u = refs
+    right_u, across, base_y, base_u, base_v, new_u, new_v, left_u = refs
     rank_cap, row_count = base_u.shape
-    row_width, col_width = row_chunks[0].shape[0], col_chunks[0].shape[0]
     n_p, n_q = n_col * row_pad, n_row * col_pad
 
     left_u[...] = jnp.zeros_like(left_u)
     for m, chunk in enumerate(row_chunks):
         left_u[m * row_pad : m * row_pad + row_width, :] = chunk[...]
-    right_u[...] = jnp.zeros_like(right_u)
-    for k, chunk in enumerate(col_chunks):
-        at = source_of(own_row[0], k, n_row)
-        right_u[pl.ds(pl.multiple_of(at * col_pad, col_pad), col_width), :] = chunk[...]
-
     total = cores[0][...].astype(jnp.float32)
     for k in range(1, n_row):
         total = total + cores[k][...].astype(jnp.float32)
@@ -170,21 +188,13 @@
     q_at = lax.broadcasted_iota(jnp.int32, (n_p, n_q), 1)
     q_at = lax.div(q_at, col_pad) * col_width + lax.rem(q_at, col_pad)
     p_chunk, p_in = lax.div(p_at, row_pad), lax.rem(p_at, row_pad)
-    p_source = lax.bitwise_xor(p_chunk, own_col[0]) if by_pairs(n_col) else p_chunk
+    p_source = lax.bitwise_xor(p_chunk, own_col) if by_pairs(n_col) else p_chunk
     p_at = p_source * row_width + p_in
     keep = (p_at < row_rank[0]) & (q_at < col_rank[0])
     core = jnp.where(keep, total, 0.0).astype(jnp.bfloat16)
 
-    old_at = lax.broadcasted_iota(jnp.int32, (rank_cap, row_count), 0)
-    kept_v = jnp.where(old_at < old_rank[0, 0], base_v[...], jnp.zeros_like(base_v))
-    new_at = lax.broadcasted_iota(jnp.int32, (half, row_count), 0)
-    probe = sketch[0:half, :]
-    probe = jnp.where(new_at < new_rank[0, 0], probe, jnp.zeros_like(probe))
-
-    left_small = dot_nt(probe, kept_v).astype(jnp.bfloat16)
-    across = dot_nt(probe, right_u[...]).astype(jnp.bfloat16)
-    middle = dot_nt(across, core).astype(jnp.bfloat16)
-    range_y = dot_nn(left_small, base_u[...]) - dot_nn(middle, left_u[...])
+    middle = dot_nt(across[...], core).astype(jnp.bfloat16)
+    range_y = base_y[...] - dot_nn(middle, left_u[...])
     diag_at = lax.broadcasted_iota(jnp.int32, (half, half), 0)
     diag_on = diag_at == lax.broadcasted_iota(jnp.int32, (half, half), 1)
     padding = jnp.where(diag_on & (diag_at >= new_rank[0, 0]), 1.0, 0.0)
@@ -194,7 +204,9 @@
     back_small = dot_nt(out_u, base_u[...]).astype(jnp.bfloat16)
     side_small = dot_nt(out_u, left_u[...]).astype(jnp.bfloat16)
     turned = dot_nn(side_small, core).astype(jnp.bfloat16)
-    summed = dot_nn(back_small, kept_v) - dot_nn(turned, right_u[...])
+    old_at = lax.broadcasted_iota(jnp.int32, (half, rank_cap), 1)
+    back_small = jnp.where(old_at < old_rank[0, 0], back_small, jnp.zeros_like(back_small))
+    summed = dot_nn(back_small, base_v[...]) - dot_nn(turned, right_u[...])
     new_u[0:half, :] = out_u
     new_v[0:half, :] = (summed / jnp.float32(row_count)).astype(jnp.bfloat16)
     if half < rank_cap:
@@ -218,8 +230,6 @@
     n_row,
     n_col,
 ):
-    own_row = jnp.reshape(lax.axis_index("row").astype(jnp.int32), (1,))
-    own_col = jnp.reshape(lax.axis_index("col").astype(jnp.int32), (1,))
     row_share, row_count = diag_inverse.shape
     rank_cap = tile_u.shape[3]
     row_width, col_width = row_v.shape[2], col_v.shape[2]
@@ -227,49 +237,47 @@
     n_p, n_q = n_col * row_pad, n_row * col_pad
     half = min(round_up(rank_cap // 2, LANES), rank_cap)
     bf16 = jnp.bfloat16
-    shape = jax.ShapeDtypeStruct
+    sizes = dict(n_row=n_row, row_pad=row_pad, col_pad=col_pad, n_col=n_col)
+    base_u, base_v = tile_u[0, 0].T, tile_v[0, 0].T
+    small = by_pairs(n_row) and by_pairs(n_col)
 
     row_chunks = spread(row_v[0].T, "row", n_row)
-    col_chunks = spread(col_v[0].T, "row", n_row)
-    right_chunks = spread(col_u[0].T, "row", n_row)
-    solved = call(
+    col_chunks = spread(jnp.concatenate([col_v[0].T, col_u[0].T], axis=0), "row", n_row)
+    (solved,) = call(
         functools.partial(row_solve_body, pad=row_pad),
-        shape((n_row * row_pad, row_share), bf16),
-        0,
-        n_row + 1,
+        [((n_row * row_pad, row_share), bf16)],
+        [],
+        [*row_chunks, diag_inverse],
         [pltpu.VMEM((n_row * row_pad, row_count), bf16)],
-    )(*row_chunks, diag_inverse)
+        small=small,
+    )
     solved = spread_near(solved, "col", n_col)
     left_chunks = spread_near(row_u[0].T, "col", n_col)
     parts = call(
-        functools.partial(core_body, n_row=n_row, n_col=n_col, row_pad=row_pad, col_pad=col_pad),
-        [shape((n_p, n_q), bf16)] * n_row,
-        1,
-        n_row + 1 + n_col,
+        functools.partial(core_body, **sizes),
+        [((n_p, n_q), bf16)] * n_row,
+        [],
+        [*col_chunks, diag_inverse, *solved],
         [pltpu.VMEM((n_q, row_count), bf16)],
-    )(own_row, *col_chunks, diag_inverse, *solved)
+        small=small,
+    )
     cores = hand_out(list(parts), "row", n_row)
+    right_u, across, base_y = call(
+        functools.partial(base_body, n_row=n_row, col_pad=col_pad, half=half),
+        [((n_q, row_count), bf16), ((half, n_q), bf16), ((half, row_count), jnp.float32)],
+        [old_rank, new_rank],
+        [*col_chunks, base_u, base_v, sketch.T],
+        small=small,
+    )
     new_u, new_v = call(
         functools.partial(
-            tile_body, n_row=n_row, n_col=n_col, row_pad=row_pad, col_pad=col_pad, half=half
+            tile_body, **sizes, row_width=row_width, col_width=col_width, half=half
         ),
-        [shape((rank_cap, row_count), bf16)] * 2,
-        6,
-        2 * n_row + n_col + 3,
-        [pltpu.VMEM((n_p, row_count), bf16), pltpu.VMEM((n_q, row_count), bf16)],
-    )(
-        own_col,
-        own_row,
-        row_rank,
-        col_rank,
-        old_rank,
-        new_rank,
-        *cores,
-        *left_chunks,
-        *right_chunks,
-        tile_u[0, 0].T,
-        tile_v[0, 0].T,
-        sketch.T,
+        [((rank_cap, row_count), bf16)] * 2,
+        [row_rank, col_rank, old_rank, new_rank],
+        [*cores, *left_chunks, right_u, across, base_y, base_u, base_v],
+        [pltpu.VMEM((n_p, row_count), bf16)],
+        small=small,
     )
     return (new_u.T[None, None], new_v.T[None, None])
 
@@ -291,4 +299,5 @@
     )
     out_specs = (P("row", "col", None, None), P("row", "col", None, None))
     body = functools.partial(on_device, n_row=mesh.shape["row"], n_col=mesh.shape["col"])
+
     return jax.shard_map(body, mesh=mesh, in_specs=in_specs, out_specs=out_specs, check_vma=False)

time: 60.1 us -> 52.3 us (0.87)
  Pallas kernels: 16.6 us -> 10.5 us
  starting transfers between devices: 27.8 us -> 25.2 us
  local copies, waits for them, and re-layouts: 1.36 us -> 2.12 us
    pallas_call x3 -> x4, Pallas kernels: 16.6 us -> 10.5 us  [call(): pl.pallas_call(body, out_shape=outs, in_specs=[pl.BlockSpec(memory_space=...]
    ppermute x26 -> x23, starting transfers between devices: 27.8 us -> 25.2 us  [swap(): return lax.ppermute(x, axis, [(i, i ^ k) for i in range(n)])]
    unnamed x54 -> x18, local copies, waits for them, and re-layouts: 1.36 us -> 2.12 us
    ppermute x26 -> x23, waiting for transfers between devices: 10.6 us -> 10.9 us  [swap(): return lax.ppermute(x, axis, [(i, i ^ k) for i in range(n)])]
  transfers between devices with their start and end apart: 26 -> 23, of which waited for: 6 -> 9; matrix products, arithmetic and copies ran while one was open for 0% -> 0% of each run, Pallas kernels for 10% -> 5%
where the time goes in v2:
time: 52.3 us; the launch traced here: 52 us
  starting transfers between devices  25.2 us (48%)
  waiting for transfers between devices  10.9 us (21%)
  Pallas kernels  10.5 us (20%)
  between operations  3.35 us (6%)
  local copies, waits for them, and re-layouts  2.12 us (4%)
    ppermute x23, starting transfers between devices, swap(): return lax.ppermute(x, axis, [(i, i ^ k) for i in range(n)])  25.2 us
    ppermute x23, waiting for transfers between devices, swap(): return lax.ppermute(x, axis, [(i, i ^ k) for i in range(n)])  10.9 us
    pallas_call x4, Pallas kernels, call(): pl.pallas_call(body, out_shape=outs, in_specs=[pl.BlockSpec(memory_space=...  10.5 us
    unnamed x18, local copies, waits for them, and re-layouts  2.12 us
  transfers between devices with their start and end apart: 23, of which 9 were waited for; matrix products, arithmetic and copies ran while one was open for 0% of the time, Pallas kernels for 5%

profile of v2, /device:TPU:0, one launch (start us, length us, event | category | flops | bytes accessed | tf_op | source)
XLA Modules:
  0.0 52.0 jit_solution(10781695853841047620)
XLA Ops:
  0.6 4.0 %collective-permute-start.5 = (bf16[28,1376]{1,0:T(8,128)(2,1)}, bf16[28,1376]{1,0:T(8,128)(2,1)S(1)}, u32[]{:S(2)}, u32[]{:S(2)}) collective-permute-start(bf16[28,1376]{1,0:T(8,128)(2,1)} %bitcast.30), channel_id=1, source_target_pairs={{0,24},{8,16},{16,8},{24,0},{1,25},{9,17},{17,9},{25,1},{2,26},{10... | collective-permute-start | bytes 231176 | tf_op jit(solution)/shard_map/ppermute | solution.py:36
  4.6 0.5 collective-permute-start.4
  5.1 0.1 collective-permute-start.3
  5.3 4.0 %collective-permute-start.21 = (bf16[28,1376]{1,0:T(8,128)(2,1)}, bf16[28,1376]{1,0:T(8,128)(2,1)S(1)}, u32[]{:S(2)}, u32[]{:S(2)}) collective-permute-start(bf16[28,1376]{1,0:T(8,128)(2,1)} %bitcast.34), channel_id=1, source_target_pairs={{0,6},{1,7},{2,4},{3,5},{4,2},{5,3},{6,0},{7,1},{8,14},{9,15},{10,... | collective-permute-start | bytes 231176 | tf_op jit(solution)/shard_map/ppermute | solution.py:36
  9.3 0.0 collective-permute-done.5.refs_3_
  9.3 0.1 collective-permute-done.4.refs_2_
  9.4 0.5 collective-permute-done.3.refs_1_
  9.9 1.2 %copy-done = bf16[344,1376]{1,0:T(8,128)(2,1)S(1)} copy-done((bf16[344,1376]{1,0:T(8,128)(2,1)S(1)}, bf16[344,1376]{1,0:T(8,128)(2,1)}, u32[]{:S(2)}) %copy-start) | copy-done | bytes 946712
  11.1 0.9 %copy-done.5 = bf16[1,1376,28]{1,2,0:T(8,128)(2,1)S(1)} copy-done((bf16[1,1376,28]{1,2,0:T(8,128)(2,1)S(1)}, bf16[1,1376,28]{1,2,0:T(8,128)(2,1)}, u32[]{:S(2)}) %copy-start.5) | copy-done | bytes 77080
  12.0 0.5 shard_map.131.refs_5_
  12.4 3.7 %collective-permute-start.11 = (bf16[128,344]{1,0:T(8,128)(2,1)S(1)}, bf16[128,344]{1,0:T(8,128)(2,1)S(1)}, u32[]{:S(2)}, u32[]{:S(2)}) collective-permute-start(bf16[128,344]{1,0:T(8,128)(2,1)S(1)} %shard_map.131.refs_5_), channel_id=1, source_target_pairs={{0,6},{1,7},{2,4},{3,5},{4,2},{5,3},{6,0},{7,1},{8,14},{9,15},{10,... | collective-permute-start | bytes 264200 | tf_op jit(solution)/shard_map/ppermute | solution.py:36
  16.1 0.0 collective-permute-start.9
  16.1 0.8 %collective-permute-start.7 = (bf16[128,344]{1,0:T(8,128)(2,1)S(1)}, bf16[128,344]{1,0:T(8,128)(2,1)S(1)}, u32[]{:S(2)}, u32[]{:S(2)}) collective-permute-start(bf16[128,344]{1,0:T(8,128)(2,1)S(1)} %shard_map.131.refs_5_), channel_id=1, source_target_pairs={{0,2},{1,3},{2,0},{3,1},{4,6},{5,7},{6,4},{7,5},{8,10},{9,11},{10,... | collective-permute-start | bytes 264200 | tf_op jit(solution)/shard_map/ppermute | solution.py:36
  16.9 0.0 copy-start.2
  16.9 0.0 copy-start.3
  16.9 0.0 copy-start.4
  16.9 1.9 %collective-permute-start.2 = (bf16[112,1376]{1,0:T(8,128)(2,1)S(1)}, bf16[112,1376]{1,0:T(8,128)(2,1)S(1)}, u32[]{:S(2)}, u32[]{:S(2)}) collective-permute-start(bf16[112,1376]{1,0:T(8,128)(2,1)S(1)} %pad_maximum_fusion.refs_0_.refs_2_), channel_id=1, source_target_pairs={{0,24},{8,16},{16,8},{24,0},{1,25},{9,17},{17,9},{25,1},{2,26},{10... | collective-permute-start | bytes 924680 | tf_op jit(solution)/shard_map/ppermute | solution.py:36
  18.9 0.0 collective-permute-done.21.refs_14_
  18.9 0.9 %collective-permute-start.1 = (bf16[112,1376]{1,0:T(8,128)(2,1)S(1)}, bf16[112,1376]{1,0:T(8,128)(2,1)S(1)}, u32[]{:S(2)}, u32[]{:S(2)}) collective-permute-start(bf16[112,1376]{1,0:T(8,128)(2,1)S(1)} %pad_maximum_fusion.refs_0_.refs_2_), channel_id=1, source_target_pairs={{0,16},{8,24},{16,0},{24,8},{1,17},{9,25},{17,1},{25,9},{2,18},{10... | collective-permute-start | bytes 924680 | tf_op jit(solution)/shard_map/ppermute | solution.py:36
  19.7 0.2 collective-permute-done.11.refs_11_
  19.9 1.1 %collective-permute-start = (bf16[112,1376]{1,0:T(8,128)(2,1)S(1)}, bf16[112,1376]{1,0:T(8,128)(2,1)S(1)}, u32[]{:S(2)}, u32[]{:S(2)}) collective-permute-start(bf16[112,1376]{1,0:T(8,128)(2,1)S(1)} %pad_maximum_fusion.refs_0_.refs_2_), channel_id=1, source_target_pairs={{0,8},{8,0},{16,24},{24,16},{1,9},{9,1},{17,25},{25,17},{2,10},{10... | collective-permute-start | bytes 924680 | tf_op jit(solution)/shard_map/ppermute | solution.py:36
  21.0 2.9 %collective-permute-done.9.refs_9_ = bf16[128,344]{1,0:T(8,128)(2,1)S(1)} collective-permute-done((bf16[128,344]{1,0:T(8,128)(2,1)S(1)}, bf16[128,344]{1,0:T(8,128)(2,1)S(1)}, u32[]{:S(2)}, u32[]{:S(2)}) %collective-permute-start.9) | collective-permute-done | bytes 88096 | tf_op jit(solution)/shard_map/ppermute | solution.py:36
  23.9 0.5 collective-permute-start.12
  24.4 0.8 %collective-permute-done.6.refs_6_ = bf16[128,344]{1,0:T(8,128)(2,1)S(1)} collective-permute-done((bf16[128,344]{1,0:T(8,128)(2,1)S(1)}, bf16[128,344]{1,0:T(8,128)(2,1)S(1)}, u32[]{:S(2)}, u32[]{:S(2)}) %collective-permute-start.6) | collective-permute-done | bytes 88096 | tf_op jit(solution)/shard_map/ppermute | solution.py:36
  25.2 0.2 collective-permute-start.10
  25.4 0.0 collective-permute-done.12.refs_12_
  25.4 0.4 collective-permute-start.8
  25.7 0.8 %collective-permute-done.10.refs_10_ = bf16[128,344]{1,0:T(8,128)(2,1)S(1)} collective-permute-done((bf16[128,344]{1,0:T(8,128)(2,1)S(1)}, bf16[128,344]{1,0:T(8,128)(2,1)S(1)}, u32[]{:S(2)}, u32[]{:S(2)}) %collective-permute-start.10) | collective-permute-done | bytes 88096 | tf_op jit(solution)/shard_map/ppermute | solution.py:36
  26.5 2.2 %collective-permute-start.19 = (bf16[28,1376]{1,0:T(8,128)(2,1)S(1)}, bf16[28,1376]{1,0:T(8,128)(2,1)S(1)}, u32[]{:S(2)}, u32[]{:S(2)}) collective-permute-start(bf16[28,1376]{1,0:T(8,128)(2,1)S(1)} %bitcast.35), channel_id=1, source_target_pairs={{0,4},{1,5},{2,6},{3,7},{4,0},{5,1},{6,2},{7,3},{8,12},{9,13},{10,... | collective-permute-start | bytes 231176 | tf_op jit(solution)/shard_map/ppermute | solution.py:36
  28.7 0.0 collective-permute-done.8.refs_8_
  28.7 0.9 %collective-permute-start.17 = (bf16[28,1376]{1,0:T(8,128)(2,1)S(1)}, bf16[28,1376]{1,0:T(8,128)(2,1)S(1)}, u32[]{:S(2)}, u32[]{:S(2)}) collective-permute-start(bf16[28,1376]{1,0:T(8,128)(2,1)S(1)} %bitcast.36), channel_id=1, source_target_pairs={{0,2},{1,3},{2,0},{3,1},{4,6},{5,7},{6,4},{7,5},{8,10},{9,11},{10,... | collective-permute-start | bytes 231176 | tf_op jit(solution)/shard_map/ppermute | solution.py:36
  29.6 3.1 %collective-permute-done.1.refs_2_.refs_4_ = bf16[112,1376]{1,0:T(8,128)(2,1)S(1)} collective-permute-done((bf16[112,1376]{1,0:T(8,128)(2,1)S(1)}, bf16[112,1376]{1,0:T(8,128)(2,1)S(1)}, u32[]{:S(2)}, u32[]{:S(2)}) %collective-permute-start.1) | collective-permute-done | bytes 308256 | tf_op jit(solution)/shard_map/ppermute | solution.py:36
  32.7 0.0 collective-permute-start.22
  32.7 0.2 collective-permute-done.refs_1_.refs_3_
  33.0 1.2 %shard_map.132 = (bf16[256,256]{1,0:T(8,128)(2,1)S(1)}, bf16[256,256]{1,0:T(8,128)(2,1)S(1)}, bf16[256,256]{1,0:T(8,128)(2,1)S(1)}, bf16[256,256]{1,0:T(8,128)(2,1)S(1)}) custom-call(bf16[112,1376]{1,0:T(8,128)(2,1)S(1)} %pad_maximum_fusion.refs_0_.refs_2_, bf16[112,1376]{1,0:T(8,128)(2,1)S(1)} %collective-permute-done.refs_1_.refs_3_, ...), custom_call_target="tpu_custom_call" | custom-call | tf_op jit(solution)/shard_map/pallas_call | solution.py:71
  34.2 1.5 %collective-permute-start.13 = (bf16[256,256]{1,0:T(8,128)(2,1)S(1)}, bf16[256,256]{1,0:T(8,128)(2,1)S(1)}, u32[]{:S(2)}, u32[]{:S(2)}) collective-permute-start(bf16[256,256]{1,0:T(8,128)(2,1)S(1)} %get-tuple-element.12), channel_id=1, source_target_pairs={{0,8},{8,0},{16,24},{24,16},{1,9},{9,1},{17,25},{25,17},{2,10},{10... | collective-permute-start | bytes 393224 | tf_op jit(solution)/shard_map/ppermute | solution.py:36
  35.7 0.6 %collective-permute-start.14 = (bf16[256,256]{1,0:T(8,128)(2,1)S(1)}, bf16[256,256]{1,0:T(8,128)(2,1)S(1)}, u32[]{:S(2)}, u32[]{:S(2)}) collective-permute-start(bf16[256,256]{1,0:T(8,128)(2,1)S(1)} %get-tuple-element.13), channel_id=1, source_target_pairs={{0,16},{8,24},{16,0},{24,8},{1,17},{9,25},{17,1},{25,9},{2,18},{10... | collective-permute-start | bytes 393224 | tf_op jit(solution)/shard_map/ppermute | solution.py:36
  36.3 0.0 collective-permute-done.17.refs_10_
  36.3 1.5 %collective-permute-start.15 = (bf16[256,256]{1,0:T(8,128)(2,1)S(1)}, bf16[256,256]{1,0:T(8,128)(2,1)S(1)}, u32[]{:S(2)}, u32[]{:S(2)}) collective-permute-start(bf16[256,256]{1,0:T(8,128)(2,1)S(1)} %get-tuple-element.14), channel_id=1, source_target_pairs={{0,24},{8,16},{16,8},{24,0},{1,25},{9,17},{17,9},{25,1},{2,26},{10... | collective-permute-start | bytes 393224 | tf_op jit(solution)/shard_map/ppermute | solution.py:36
  37.8 0.0 collective-permute-done.16.refs_9_
  37.8 0.0 collective-permute-start.20
  37.8 0.0 collective-permute-done.22.refs_15_
  37.8 0.5 collective-permute-start.18
  40.9 0.8 %shard_map.133 = (bf16[256,1376]{1,0:T(8,128)(2,1)S(1)}, bf16[128,256]{1,0:T(8,128)(2,1)S(1)}, f32[128,1376]{1,0:T(8,128)S(1)}) custom-call(s32[1,1]{1,0:T(1,128)S(6)} %copy.16.refs_0_.refs_2_, s32[1,1]{1,0:T(1,128)S(6)} %copy.17.refs_1_.refs_3_, bf16[112,1376]{1,0:T(8,128)(2,1)S(1)} %pad_maximum_fusion.refs_0_.refs_2_, ...), custom_call_target="tpu_custom_call" | custom-call | tf_op jit(solution)/shard_map/pallas_call | solution.py:71
  41.8 0.0 collective-permute-done.20.refs_13_
  41.8 0.0 collective-permute-done.13.refs_5_
  41.8 2.3 %collective-permute-done.14.refs_6_ = bf16[256,256]{1,0:T(8,128)(2,1)S(1)} collective-permute-done((bf16[256,256]{1,0:T(8,128)(2,1)S(1)}, bf16[256,256]{1,0:T(8,128)(2,1)S(1)}, u32[]{:S(2)}, u32[]{:S(2)}) %collective-permute-start.14) | collective-permute-done | bytes 131104 | tf_op jit(solution)/shard_map/ppermute | solution.py:36
  44.1 7.9 %shard_map.134 = (bf16[224,1376]{1,0:T(8,128)(2,1)}, bf16[224,1376]{1,0:T(8,128)(2,1)}) custom-call(s32[1]{0:T(128)S(6)} %copy.14.refs_0_, s32[1]{0:T(128)S(6)} %copy.15.refs_1_, s32[1,1]{1,0:T(1,128)S(6)} %copy.16.refs_0_.refs_2_, s32[1,1]{1,0:T(1,128)S(6)} %copy.17.refs_1_.refs_3_, bf16[256,256]{1,0:T(8,128)(2,1)S(1)} %get-tuple-element.11.refs_4_, ...), custom_call_target="tpu_custom_call" | custom-call | tf_op jit(solution)/shard_map/pallas_call | solution.py:71
  (21 shorter events, 0.1 us)
Async XLA Ops:
  0.6 8.6 %collective-permute-start.5 = (bf16[28,1376]{1,0:T(8,128)(2,1)}, bf16[28,1376]{1,0:T(8,128)(2,1)S(1)}, u32[]{:S(2)}, u32[]{:S(2)}) collective-permute-start(bf16[28,1376]{1,0:T(8,128)(2,1)} %bitcast.30), channel_id=1, source_target_pairs={{0,24},{8,16},{16,8},{24,0},{1,25},{9,17},{17,9},{25,1},{2,26},{10... | collective-permute-start | bytes 231176 | tf_op jit(solution)/shard_map/ppermute | solution.py:36
  4.6 4.8 %collective-permute-start.4 = (bf16[28,1376]{1,0:T(8,128)(2,1)}, bf16[28,1376]{1,0:T(8,128)(2,1)S(1)}, u32[]{:S(2)}, u32[]{:S(2)}) collective-permute-start(bf16[28,1376]{1,0:T(8,128)(2,1)} %bitcast.31), channel_id=1, source_target_pairs={{0,16},{8,24},{16,0},{24,8},{1,17},{9,25},{17,1},{25,9},{2,18},{10... | collective-permute-start | bytes 231176 | tf_op jit(solution)/shard_map/ppermute | solution.py:36
  5.1 4.7 %collective-permute-start.3 = (bf16[28,1376]{1,0:T(8,128)(2,1)}, bf16[28,1376]{1,0:T(8,128)(2,1)S(1)}, u32[]{:S(2)}, u32[]{:S(2)}) collective-permute-start(bf16[28,1376]{1,0:T(8,128)(2,1)} %bitcast.32), channel_id=1, source_target_pairs={{0,8},{8,0},{16,24},{24,16},{1,9},{9,1},{17,25},{25,17},{2,10},{10... | collective-permute-start | bytes 231176 | tf_op jit(solution)/shard_map/ppermute | solution.py:36
  5.3 13.6 %collective-permute-start.21 = (bf16[28,1376]{1,0:T(8,128)(2,1)}, bf16[28,1376]{1,0:T(8,128)(2,1)S(1)}, u32[]{:S(2)}, u32[]{:S(2)}) collective-permute-start(bf16[28,1376]{1,0:T(8,128)(2,1)} %bitcast.34), channel_id=1, source_target_pairs={{0,6},{1,7},{2,4},{3,5},{4,2},{5,3},{6,0},{7,1},{8,14},{9,15},{10,... | collective-permute-start | bytes 231176 | tf_op jit(solution)/shard_map/ppermute | solution.py:36
  9.9 1.2 %copy-start = (bf16[344,1376]{1,0:T(8,128)(2,1)S(1)}, bf16[344,1376]{1,0:T(8,128)(2,1)}, u32[]{:S(2)}) copy-start(bf16[344,1376]{1,0:T(8,128)(2,1)} %refs_4_.3) | copy-start | bytes 2840068
  11.1 0.9 %copy-start.5 = (bf16[1,1376,28]{1,2,0:T(8,128)(2,1)S(1)}, bf16[1,1376,28]{1,2,0:T(8,128)(2,1)}, u32[]{:S(2)}) copy-start(bf16[1,1376,28]{1,2,0:T(8,128)(2,1)} %param.14) | copy-start | bytes 231172
  12.0 4.9 %copy-start.7 = (bf16[1,1376,56]{1,2,0:T(8,128)(2,1)S(1)}, bf16[1,1376,56]{1,2,0:T(8,128)(2,1)}, u32[]{:S(2)}) copy-start(bf16[1,1376,56]{1,2,0:T(8,128)(2,1)} %param.15) | copy-start | bytes 462340
  12.0 4.9 %copy-start.8 = (bf16[1,1376,56]{1,2,0:T(8,128)(2,1)S(1)}, bf16[1,1376,56]{1,2,0:T(8,128)(2,1)}, u32[]{:S(2)}) copy-start(bf16[1,1376,56]{1,2,0:T(8,128)(2,1)} %param.16) | copy-start | bytes 462340
  12.0 21.0 %copy-start.1 = (bf16[344,1376]{1,0:T(8,128)(2,1)S(1)}, bf16[344,1376]{1,0:T(8,128)(2,1)}, u32[]{:S(2)}) copy-start(bf16[344,1376]{1,0:T(8,128)(2,1)} %refs_4_.3) | copy-start | bytes 2840068
  12.4 7.5 %collective-permute-start.11 = (bf16[128,344]{1,0:T(8,128)(2,1)S(1)}, bf16[128,344]{1,0:T(8,128)(2,1)S(1)}, u32[]{:S(2)}, u32[]{:S(2)}) collective-permute-start(bf16[128,344]{1,0:T(8,128)(2,1)S(1)} %shard_map.131.refs_5_), channel_id=1, source_target_pairs={{0,6},{1,7},{2,4},{3,5},{4,2},{5,3},{6,0},{7,1},{8,14},{9,15},{10,... | collective-permute-start | bytes 264200 | tf_op jit(solution)/shard_map/ppermute | solution.py:36
  16.1 7.8 %collective-permute-start.9 = (bf16[128,344]{1,0:T(8,128)(2,1)S(1)}, bf16[128,344]{1,0:T(8,128)(2,1)S(1)}, u32[]{:S(2)}, u32[]{:S(2)}) collective-permute-start(bf16[128,344]{1,0:T(8,128)(2,1)S(1)} %shard_map.131.refs_5_), channel_id=1, source_target_pairs={{0,4},{1,5},{2,6},{3,7},{4,0},{5,1},{6,2},{7,3},{8,12},{9,13},{10,... | collective-permute-start | bytes 264200 | tf_op jit(solution)/shard_map/ppermute | solution.py:36
  16.1 7.8 %collective-permute-start.7 = (bf16[128,344]{1,0:T(8,128)(2,1)S(1)}, bf16[128,344]{1,0:T(8,128)(2,1)S(1)}, u32[]{:S(2)}, u32[]{:S(2)}) collective-permute-start(bf16[128,344]{1,0:T(8,128)(2,1)S(1)} %shard_map.131.refs_5_), channel_id=1, source_target_pairs={{0,2},{1,3},{2,0},{3,1},{4,6},{5,7},{6,4},{7,5},{8,10},{9,11},{10,... | collective-permute-start | bytes 264200 | tf_op jit(solution)/shard_map/ppermute | solution.py:36
  16.9 9.7 %copy-start.6 = (bf16[1,1376,28]{1,2,0:T(8,128)(2,1)S(1)}, bf16[1,1376,28]{1,2,0:T(8,128)(2,1)}, u32[]{:S(2)}) copy-start(bf16[1,1376,28]{1,2,0:T(8,128)(2,1)} %param.13) | copy-start | bytes 231172
  16.9 24.0 %copy-start.2 = (bf16[1,1,1376,224]{2,3,1,0:T(8,128)(2,1)S(1)}, bf16[1,1,1376,224]{2,3,1,0:T(8,128)(2,1)}, u32[]{:S(2)}) copy-start(bf16[1,1,1376,224]{2,3,1,0:T(8,128)(2,1)} %param.17) | copy-start | bytes 1849348
  16.9 24.0 %copy-start.3 = (bf16[1,1,1376,224]{2,3,1,0:T(8,128)(2,1)S(1)}, bf16[1,1,1376,224]{2,3,1,0:T(8,128)(2,1)}, u32[]{:S(2)}) copy-start(bf16[1,1,1376,224]{2,3,1,0:T(8,128)(2,1)} %param.18) | copy-start | bytes 1849348
  16.9 24.0 %copy-start.4 = (bf16[1376,224]{0,1:T(8,128)(2,1)S(1)}, bf16[1376,224]{0,1:T(8,128)(2,1)}, u32[]{:S(2)}) copy-start(bf16[1376,224]{0,1:T(8,128)(2,1)} %param.19) | copy-start | bytes 1849348
  16.9 12.7 %collective-permute-start.2 = (bf16[112,1376]{1,0:T(8,128)(2,1)S(1)}, bf16[112,1376]{1,0:T(8,128)(2,1)S(1)}, u32[]{:S(2)}, u32[]{:S(2)}) collective-permute-start(bf16[112,1376]{1,0:T(8,128)(2,1)S(1)} %pad_maximum_fusion.refs_0_.refs_2_), channel_id=1, source_target_pairs={{0,24},{8,16},{16,8},{24,0},{1,25},{9,17},{17,9},{25,1},{2,26},{10... | collective-permute-start | bytes 924680 | tf_op jit(solution)/shard_map/ppermute | solution.py:36
  18.9 13.9 %collective-permute-start.1 = (bf16[112,1376]{1,0:T(8,128)(2,1)S(1)}, bf16[112,1376]{1,0:T(8,128)(2,1)S(1)}, u32[]{:S(2)}, u32[]{:S(2)}) collective-permute-start(bf16[112,1376]{1,0:T(8,128)(2,1)S(1)} %pad_maximum_fusion.refs_0_.refs_2_), channel_id=1, source_target_pairs={{0,16},{8,24},{16,0},{24,8},{1,17},{9,25},{17,1},{25,9},{2,18},{10... | collective-permute-start | bytes 924680 | tf_op jit(solution)/shard_map/ppermute | solution.py:36
  19.9 13.1 %collective-permute-start = (bf16[112,1376]{1,0:T(8,128)(2,1)S(1)}, bf16[112,1376]{1,0:T(8,128)(2,1)S(1)}, u32[]{:S(2)}, u32[]{:S(2)}) collective-permute-start(bf16[112,1376]{1,0:T(8,128)(2,1)S(1)} %pad_maximum_fusion.refs_0_.refs_2_), channel_id=1, source_target_pairs={{0,8},{8,0},{16,24},{24,16},{1,9},{9,1},{17,25},{25,17},{2,10},{10... | collective-permute-start | bytes 924680 | tf_op jit(solution)/shard_map/ppermute | solution.py:36
  23.9 1.3 %collective-permute-start.6 = (bf16[128,344]{1,0:T(8,128)(2,1)S(1)}, bf16[128,344]{1,0:T(8,128)(2,1)S(1)}, u32[]{:S(2)}, u32[]{:S(2)}) collective-permute-start(bf16[128,344]{1,0:T(8,128)(2,1)S(1)} %shard_map.131.refs_5_), channel_id=1, source_target_pairs={{0,1},{1,0},{2,3},{3,2},{4,5},{5,4},{6,7},{7,6},{8,9},{9,8},{10,11... | collective-permute-start | bytes 264200 | tf_op jit(solution)/shard_map/ppermute | solution.py:36
  23.9 1.5 %collective-permute-start.12 = (bf16[128,344]{1,0:T(8,128)(2,1)S(1)}, bf16[128,344]{1,0:T(8,128)(2,1)S(1)}, u32[]{:S(2)}, u32[]{:S(2)}) collective-permute-start(bf16[128,344]{1,0:T(8,128)(2,1)S(1)} %collective-permute-done.11.refs_11_), channel_id=1, source_target_pairs={{0,1},{1,0},{2,3},{3,2},{4,5},{5,4},{6,7},{7,6},{8,9},{9,8},{10,11... | collective-permute-start | bytes 264200 | tf_op jit(solution)/shard_map/ppermute | solution.py:36
  25.2 1.3 %collective-permute-start.10 = (bf16[128,344]{1,0:T(8,128)(2,1)S(1)}, bf16[128,344]{1,0:T(8,128)(2,1)S(1)}, u32[]{:S(2)}, u32[]{:S(2)}) collective-permute-start(bf16[128,344]{1,0:T(8,128)(2,1)S(1)} %collective-permute-done.9.refs_9_), channel_id=1, source_target_pairs={{0,1},{1,0},{2,3},{3,2},{4,5},{5,4},{6,7},{7,6},{8,9},{9,8},{10,11... | collective-permute-start | bytes 264200 | tf_op jit(solution)/shard_map/ppermute | solution.py:36
  25.4 3.3 %collective-permute-start.8 = (bf16[128,344]{1,0:T(8,128)(2,1)S(1)}, bf16[128,344]{1,0:T(8,128)(2,1)S(1)}, u32[]{:S(2)}, u32[]{:S(2)}) collective-permute-start(bf16[128,344]{1,0:T(8,128)(2,1)S(1)} %collective-permute-done.7.refs_7_), channel_id=1, source_target_pairs={{0,1},{1,0},{2,3},{3,2},{4,5},{5,4},{6,7},{7,6},{8,9},{9,8},{10,11... | collective-permute-start | bytes 264200 | tf_op jit(solution)/shard_map/ppermute | solution.py:36
  26.5 9.2 %collective-permute-start.19 = (bf16[28,1376]{1,0:T(8,128)(2,1)S(1)}, bf16[28,1376]{1,0:T(8,128)(2,1)S(1)}, u32[]{:S(2)}, u32[]{:S(2)}) collective-permute-start(bf16[28,1376]{1,0:T(8,128)(2,1)S(1)} %bitcast.35), channel_id=1, source_target_pairs={{0,4},{1,5},{2,6},{3,7},{4,0},{5,1},{6,2},{7,3},{8,12},{9,13},{10,... | collective-permute-start | bytes 231176 | tf_op jit(solution)/shard_map/ppermute | solution.py:36
  28.7 7.6 %collective-permute-start.17 = (bf16[28,1376]{1,0:T(8,128)(2,1)S(1)}, bf16[28,1376]{1,0:T(8,128)(2,1)S(1)}, u32[]{:S(2)}, u32[]{:S(2)}) collective-permute-start(bf16[28,1376]{1,0:T(8,128)(2,1)S(1)} %bitcast.36), channel_id=1, source_target_pairs={{0,2},{1,3},{2,0},{3,1},{4,6},{5,7},{6,4},{7,5},{8,10},{9,11},{10,... | collective-permute-start | bytes 231176 | tf_op jit(solution)/shard_map/ppermute | solution.py:36
  29.6 8.2 %collective-permute-start.16 = (bf16[28,1376]{1,0:T(8,128)(2,1)S(1)}, bf16[28,1376]{1,0:T(8,128)(2,1)S(1)}, u32[]{:S(2)}, u32[]{:S(2)}) collective-permute-start(bf16[28,1376]{1,0:T(8,128)(2,1)S(1)} %bitcast.37), channel_id=1, source_target_pairs={{0,1},{1,0},{2,3},{3,2},{4,5},{5,4},{6,7},{7,6},{8,9},{9,8},{10,11... | collective-permute-start | bytes 231176 | tf_op jit(solution)/shard_map/ppermute | solution.py:36
  32.7 5.1 %collective-permute-start.22 = (bf16[28,1376]{1,0:T(8,128)(2,1)S(1)}, bf16[28,1376]{1,0:T(8,128)(2,1)S(1)}, u32[]{:S(2)}, u32[]{:S(2)}) collective-permute-start(bf16[28,1376]{1,0:T(8,128)(2,1)S(1)} %collective-permute-done.21.refs_14_), channel_id=1, source_target_pairs={{0,1},{1,0},{2,3},{3,2},{4,5},{5,4},{6,7},{7,6},{8,9},{9,8},{10,11... | collective-permute-start | bytes 231176 | tf_op jit(solution)/shard_map/ppermute | solution.py:36
  34.2 7.6 %collective-permute-start.13 = (bf16[256,256]{1,0:T(8,128)(2,1)S(1)}, bf16[256,256]{1,0:T(8,128)(2,1)S(1)}, u32[]{:S(2)}, u32[]{:S(2)}) collective-permute-start(bf16[256,256]{1,0:T(8,128)(2,1)S(1)} %get-tuple-element.12), channel_id=1, source_target_pairs={{0,8},{8,0},{16,24},{24,16},{1,9},{9,1},{17,25},{25,17},{2,10},{10... | collective-permute-start | bytes 393224 | tf_op jit(solution)/shard_map/ppermute | solution.py:36
  35.7 8.4 %collective-permute-start.14 = (bf16[256,256]{1,0:T(8,128)(2,1)S(1)}, bf16[256,256]{1,0:T(8,128)(2,1)S(1)}, u32[]{:S(2)}, u32[]{:S(2)}) collective-permute-start(bf16[256,256]{1,0:T(8,128)(2,1)S(1)} %get-tuple-element.13), channel_id=1, source_target_pairs={{0,16},{8,24},{16,0},{24,8},{1,17},{9,25},{17,1},{25,9},{2,18},{10... | collective-permute-start | bytes 393224 | tf_op jit(solution)/shard_map/ppermute | solution.py:36
  36.3 7.8 %collective-permute-start.15 = (bf16[256,256]{1,0:T(8,128)(2,1)S(1)}, bf16[256,256]{1,0:T(8,128)(2,1)S(1)}, u32[]{:S(2)}, u32[]{:S(2)}) collective-permute-start(bf16[256,256]{1,0:T(8,128)(2,1)S(1)} %get-tuple-element.14), channel_id=1, source_target_pairs={{0,24},{8,16},{16,8},{24,0},{1,25},{9,17},{17,9},{25,1},{2,26},{10... | collective-permute-start | bytes 393224 | tf_op jit(solution)/shard_map/ppermute | solution.py:36
  37.8 4.0 %collective-permute-start.20 = (bf16[28,1376]{1,0:T(8,128)(2,1)S(1)}, bf16[28,1376]{1,0:T(8,128)(2,1)S(1)}, u32[]{:S(2)}, u32[]{:S(2)}) collective-permute-start(bf16[28,1376]{1,0:T(8,128)(2,1)S(1)} %collective-permute-done.19.refs_12_), channel_id=1, source_target_pairs={{0,1},{1,0},{2,3},{3,2},{4,5},{5,4},{6,7},{7,6},{8,9},{9,8},{10,11... | collective-permute-start | bytes 231176 | tf_op jit(solution)/shard_map/ppermute | solution.py:36
  37.8 4.0 %collective-permute-start.18 = (bf16[28,1376]{1,0:T(8,128)(2,1)S(1)}, bf16[28,1376]{1,0:T(8,128)(2,1)S(1)}, u32[]{:S(2)}, u32[]{:S(2)}) collective-permute-start(bf16[28,1376]{1,0:T(8,128)(2,1)S(1)} %collective-permute-done.17.refs_10_), channel_id=1, source_target_pairs={{0,1},{1,0},{2,3},{3,2},{4,5},{5,4},{6,7},{7,6},{8,9},{9,8},{10,11... | collective-permute-start | bytes 231176 | tf_op jit(solution)/shard_map/ppermute | solution.py:36
